TPU v7x, 128 devices: a whole 4x4x4 slice. The times are simulated.
128 devices in a mesh: tp: 2 (over core), sp: 64 (over z, y, x).
Axes of the slice: x: 4, y: 4, z: 4, core: 2. Of those that a mesh axis runs over, the one named last changes fastest.
Arguments:
- x_tok: bfloat16 [96, 3072], replicated
- seq_lens: int32 [96], replicated
- k_cache: bfloat16 [96, 1024, 8, 128], P(None, 'sp', 'tp')
- v_cache: bfloat16 [96, 1024, 8, 128], P(None, 'sp', 'tp')
- g_attn: bfloat16 [3072], replicated
- w_q: bfloat16 [3072, 3072], P(None, 'tp')
- w_k: bfloat16 [3072, 1024], P(None, 'tp')
- w_v: bfloat16 [3072, 1024], P(None, 'tp')
- w_o: bfloat16 [3072, 3072], P('tp')
- g_mlp: bfloat16 [3072], replicated
- w_gate: bfloat16 [3072, 8192], P(None, 'tp')
- w_up: bfloat16 [3072, 8192], P(None, 'tp')
- w_down: bfloat16 [8192, 3072], P('tp')
Outputs:
- output 1: bfloat16 [96, 3072], replicated
- output 2: bfloat16 [96, 1024, 8, 128], P(None, 'sp', 'tp')
- output 3: bfloat16 [96, 1024, 8, 128], P(None, 'sp', 'tp')
All inputs are finite; a program needn't handle non-finite values.
Results may differ from a plain program's by a relative error of at most 0.0137389.
Values sent between devices are 32-bit elements.
A program may use at most 1 GiB of HBM per device.

v0:
```python
import jax
import jax.numpy as jnp
from jax import lax
from jax.sharding import PartitionSpec as P

ROPE_BASE = 500000.0
NORM_EPS = 1e-5


def rms_norm(x_in, norm_gain):
    x_f32 = x_in.astype(jnp.float32)
    inv_rms = lax.rsqrt(jnp.mean(x_f32 * x_f32, axis=-1, keepdims=True) + NORM_EPS)
    return (x_f32 * inv_rms * norm_gain.astype(jnp.float32)).astype(jnp.bfloat16)


def apply_rope(heads_in, positions):
    head_dim = heads_in.shape[-1]
    half_dim = head_dim // 2
    inv_freq = jnp.power(jnp.float32(ROPE_BASE), jnp.arange(half_dim, dtype=jnp.float32) * (-2.0 / head_dim))
    angles = positions.astype(jnp.float32)[:, None, None] * inv_freq
    cos_a = jnp.cos(angles)
    sin_a = jnp.sin(angles)
    heads_f32 = heads_in.astype(jnp.float32)
    first_half = heads_f32[..., :half_dim]
    second_half = heads_f32[..., half_dim:]
    rotated = jnp.concatenate([first_half * cos_a - second_half * sin_a, second_half * cos_a + first_half * sin_a], axis=-1)
    return rotated.astype(jnp.bfloat16)


def solution(mesh):
    cache_spec = P(None, "sp", "tp", None)
    col_spec = P(None, "tp")
    row_spec = P("tp", None)
    full_spec = P()

    def local_step(x_tok, seq_lens, k_blk, v_blk, g_attn, wq_loc, wk_loc, wv_loc, wo_loc, g_mlp, wg_loc, wu_loc, wd_loc):
        batch_rows, seq_blk, kv_loc, head_dim = k_blk.shape
        q_loc = wq_loc.shape[1] // head_dim
        groups = q_loc // kv_loc
        x_norm = rms_norm(x_tok, g_attn)
        q_new = jnp.dot(x_norm, wq_loc, preferred_element_type=jnp.float32).astype(jnp.bfloat16).reshape(batch_rows, q_loc, head_dim)
        k_new = jnp.dot(x_norm, wk_loc, preferred_element_type=jnp.float32).astype(jnp.bfloat16).reshape(batch_rows, kv_loc, head_dim)
        v_new = jnp.dot(x_norm, wv_loc, preferred_element_type=jnp.float32).astype(jnp.bfloat16).reshape(batch_rows, kv_loc, head_dim)
        q_rot = apply_rope(q_new, seq_lens)
        k_rot = apply_rope(k_new, seq_lens)
        local_pos = lax.axis_index("sp") * seq_blk + jnp.arange(seq_blk)
        is_new = (local_pos[None, :] == seq_lens[:, None])[:, :, None, None]
        k_out = jnp.where(is_new, k_rot[:, None], k_blk)
        v_out = jnp.where(is_new, v_new[:, None], v_blk)
        q_grp = q_rot.reshape(batch_rows, kv_loc, groups, head_dim)
        scores = jnp.einsum("bkgd,bskd->bkgs", q_grp, k_out, preferred_element_type=jnp.float32) * (head_dim ** -0.5)
        is_valid = (local_pos[None, :] <= seq_lens[:, None])[:, None, None, :]
        masked = jnp.where(is_valid, scores, -1e30)
        blk_max = jnp.max(masked, axis=-1, keepdims=True)
        weights = jnp.where(is_valid, jnp.exp(masked - blk_max), 0.0)
        blk_sum = jnp.sum(weights, axis=-1, keepdims=True)
        blk_mix = jnp.einsum("bkgs,bskd->bkgd", weights.astype(jnp.bfloat16), v_out, preferred_element_type=jnp.float32)
        glob_max = lax.pmax(blk_max, "sp")
        factor = jnp.exp(blk_max - glob_max)
        packed = lax.psum(jnp.concatenate([blk_mix * factor, blk_sum * factor], axis=-1), "sp")
        attn_out = (packed[..., :head_dim] / packed[..., head_dim:]).astype(jnp.bfloat16).reshape(batch_rows, q_loc * head_dim)
        attn_proj = lax.psum(jnp.dot(attn_out, wo_loc, preferred_element_type=jnp.float32), "tp")
        hidden = (x_tok.astype(jnp.float32) + attn_proj).astype(jnp.bfloat16)
        h_norm = rms_norm(hidden, g_mlp)
        gate_proj = jnp.dot(h_norm, wg_loc, preferred_element_type=jnp.float32).astype(jnp.bfloat16)
        up_proj = jnp.dot(h_norm, wu_loc, preferred_element_type=jnp.float32).astype(jnp.bfloat16)
        act_prod = (jax.nn.silu(gate_proj.astype(jnp.float32)) * up_proj.astype(jnp.float32)).astype(jnp.bfloat16)
        mlp_out = lax.psum(jnp.dot(act_prod, wd_loc, preferred_element_type=jnp.float32), "tp")
        y_out = (hidden.astype(jnp.float32) + mlp_out).astype(jnp.bfloat16)
        return y_out, k_out, v_out

    return jax.shard_map(local_step, mesh=mesh, in_specs=(full_spec, full_spec, cache_spec, cache_spec, full_spec, col_spec, col_spec, col_spec, row_spec, full_spec, col_spec, col_spec, row_spec), out_specs=(full_spec, cache_spec, cache_spec), check_vma=False)
```

profile of v0, /device:TPU:1, one launch (start us, length us, event | category | flops | bytes accessed | tf_op | source)
XLA Modules:
  0.0 449.3 jit_solution(8490709151112061916)
XLA Ops:
  7.2 0.0 copy-start
  7.2 0.0 all-reduce.4.cloned.1.call-start
  7.3 0.8 convert_element_type.85
  8.1 1.3 fusion.24
  9.4 0.7 convert_element_type.80
  10.1 1.3 broadcast_compare_fusion.1
  11.5 0.0 copy-done
  11.5 1.7 convolution_convert_fusion.3
  13.3 0.0 copy-start.2
  13.3 2.8 fusion.32
  16.1 0.1 reshape.169
  16.2 0.0 copy-done.2
  16.2 5.4 %fusion.5 = f32[96,1536]{1,0:T(8,128)S(1)} fusion(bf16[3072,1536]{1,0:T(8,128)(2,1)} %param.18, bf16[96,3072]{1,0:T(8,128)(2,1)S(1)} %copy-done.2, f32[3072]{0:T(1024)S(1)} %convert_element_type.80, f32[96]{0:T(128)S(1)} %add_rsqrt_fusion.1), kind=kOutput, calls=%fused_computation.8 | convolution fusion | flops 907444224 | bytes 10629504 | tf_op jit(solution)/shard_map/dot_general | solution.py:41
  21.5 0.1 reshape.168
  21.7 0.2 multiply_cosine_fusion
  21.9 0.2 subtract_convert_fusion.1
  22.1 0.4 subtract_convert_fusion
  22.5 0.0 copy-start.7
  22.5 0.3 copy.47
  22.8 0.3 copy.49
  23.2 0.3 copy.48
  23.5 0.3 copy.50
  23.8 0.1 pad_maximum_fusion.1
  24.0 0.0 copy-done.7
  24.0 5.7 %broadcast_select_fusion = (bf16[96,16,4,128]{3,2,1,0:T(4,128)(2,1)S(1)}, bf16[96,16,4,128]{3,2,1,0:T(4,128)(2,1)S(1)}) fusion(bf16[96,16,4,128]{3,2,1,0:T(4,128)(2,1)} %param.16, pred[96,16]{1,0:T(8,128)(4,1)S(1)} %copy-done.7, bf16[96,4,128]{2,1,0:T(4,128)(2,1)S(1)} %broadcast_in_dim.70, bf16[96,16,4,128]{3,2,1,0:T(4,128)(2,1)} %param.15, ...), kind=kLoop, calls=%fused_computation.25 | loop fusion | flops 1572864 | bytes 6489600 | tf_op jit(solution)/shard_map/jit(_where)/select_n | solution.py:49
  29.7 0.0 copy-start.6
  29.7 0.0 copy-start.5
  29.7 2.1 fusion.55
  31.9 0.0 copy-done.6
  31.9 0.1 copy.53
  32.0 155.4 %pmax.7 = f32[96,4,3,1]{0,1,3,2:T(4,128)S(1)} all-reduce(f32[96,4,3,1]{0,1,3,2:T(4,128)S(1)} %bitcast.22), channel_id=1, replica_groups=mesh['tp'=2,'sp'=64] {'sp'}, use_global_device_ids=true, to_apply=%region_2.3 | all-reduce | flops 1152 | bytes 9216 | tf_op jit(solution)/shard_map/pmax | solution.py:58
  187.4 2.1 fusion.35
  189.5 0.1 copy.55
  189.7 0.2 copy.54
  189.8 0.5 copy.56
  190.3 0.0 copy-done.5
  190.3 2.1 fusion.18
  192.5 1.6 pad_maximum_fusion
  194.0 0.0 all-reduce.4.cloned.1.call-update
  194.1 0.2 all-reduce.6.cloned.1.call-start
  194.3 151.6 %all-reduce.4.cloned.1.call-done = f32[96,4,3,129]{3,2,1,0:T(4,128)} async-done(((f32[96,4,3,129]{3,2,1,0:T(4,128)}), f32[96,4,3,129]{3,2,1,0:T(4,128)}) %all-reduce.4.cloned.1.call-update) | async-done | bytes 594448 | tf_op jit(solution)/shard_map/psum | solution.py:60
  345.9 0.0 slice-start
  345.9 0.0 copy-start.4
  345.9 1.1 slice-done
  347.1 2.4 copy.59
  349.4 0.0 copy-done.4
  349.4 0.5 fusion.34
  349.9 0.3 reshape.167
  350.2 0.0 copy-start.8
  350.2 6.3 %fusion.56 = f32[96,3072]{1,0:T(8,128)} fusion(bf16[96,1536]{1,0:T(8,128)(2,1)S(1)} %reshape.167, bf16[1536,3072]{1,0:T(8,128)(2,1)} %param.21), kind=kOutput, calls=%fused_computation.73 | convolution fusion | flops 905969664 | bytes 10911744 | tf_op jit(solution)/shard_map/dot_general | solution.py:62
  356.5 0.0 all-reduce.6.cloned.1.call-update
  356.6 0.0 all-reduce.8.cloned.1.call-start
  356.6 0.0 copy-done.8
  356.6 24.6 %all-reduce.6.cloned.1.call-done = f32[96,3072]{1,0:T(8,128)} async-done(((f32[96,3072]{1,0:T(8,128)}), f32[96,3072]{1,0:T(8,128)}) %all-reduce.6.cloned.1.call-update) | async-done | bytes 1179664 | tf_op jit(solution)/shard_map/psum | solution.py:62
  381.3 1.5 fusion.28
  382.8 0.0 copy-start.3
  382.8 10.6 %fusion.3 = f32[96,4096]{1,0:T(8,128)S(1)} fusion(bf16[3072,4096]{1,0:T(8,128)(2,1)} %param.23, bf16[96,3072]{1,0:T(8,128)(2,1)S(1)} %get-tuple-element.4, f32[3072]{0:T(1024)S(1)} %convert_element_type.94, f32[96]{0:T(128)S(1)} %add_rsqrt_fusion), kind=kOutput, calls=%fused_computation.5 | convolution fusion | flops 2417885184 | bytes 27341184 | tf_op jit(solution)/shard_map/dot_general | solution.py:65
  393.4 0.0 copy-done.3
  393.4 20.6 %fusion.4 = f32[96,3072]{1,0:T(8,128)} fusion(bf16[4096,3072]{1,0:T(8,128)(2,1)} %param.25, bf16[3072,4096]{1,0:T(8,128)(2,1)} %param.24, f32[96,4096]{1,0:T(8,128)S(1)} %fusion.3, bf16[96,3072]{1,0:T(8,128)(2,1)S(1)} %get-tuple-element.4, f32[3072]{0:T(1024)S(1)} %convert_element_type.94, f32[96]{0:T(128)S(1)} %add_rsqrt_fusion), kind=kOutput, calls=%fused_computation.6 | convolution fusion | flops 4836163584 | bytes 53686656 | tf_op jit(solution)/shard_map/dot_general | solution.py:68
  414.1 0.0 copy-start.1
  414.1 0.0 all-reduce.8.cloned.1.call-update
  414.1 26.3 %all-reduce.8.cloned.1.call-done = f32[96,3072]{1,0:T(8,128)} async-done(((f32[96,3072]{1,0:T(8,128)}), f32[96,3072]{1,0:T(8,128)}) %all-reduce.8.cloned.1.call-update) | async-done | bytes 1179664 | tf_op jit(solution)/shard_map/psum | solution.py:68
  440.4 2.3 fusion.31
  442.8 0.0 copy-done.1
  (7 shorter events, 0.1 us)
Async XLA Ops:
  7.2 4.3 copy-start
  7.2 338.7 %all-reduce.4.cloned.1.call-start = ((), (), s32[]{:S(2)}) async-start(), calls=%async_computation | async-start | bytes 3145728 | tf_op jit(solution)/shard_map/psum | solution.py:60
  13.3 2.9 copy-start.2
  22.5 1.5 copy-start.7
  29.7 2.2 copy-start.6
  29.7 160.6 %copy-start.5 = (bf16[96,16,4,128]{3,2,1,0:T(4,128)(2,1)}, bf16[96,16,4,128]{3,2,1,0:T(4,128)(2,1)S(1)}, u32[]{:S(2)}) copy-start(bf16[96,16,4,128]{3,2,1,0:T(4,128)(2,1)S(1)} %get-tuple-element.11) | copy-start | bytes 4718596
  194.1 187.2 %all-reduce.6.cloned.1.call-start = ((), (), s32[]{:S(2)}) async-start(), calls=%async_computation.1 | async-start | bytes 2359296 | tf_op jit(solution)/shard_map/psum | solution.py:62
  345.9 1.1 slice-start
  345.9 3.5 copy-start.4
  350.2 6.4 %copy-start.8 = (bf16[3072]{0:T(1024)(128)(2,1)S(1)}, bf16[3072]{0:T(1024)(128)(2,1)}, u32[]{:S(2)}) copy-start(bf16[3072]{0:T(1024)(128)(2,1)} %param.22) | copy-start | bytes 18436
  356.6 83.8 %all-reduce.8.cloned.1.call-start = ((), (), s32[]{:S(2)}) async-start(), calls=%async_computation.2 | async-start | bytes 2359296 | tf_op jit(solution)/shard_map/psum | solution.py:68
  382.8 10.6 %copy-start.3 = (bf16[96,3072]{1,0:T(8,128)(2,1)}, bf16[96,3072]{1,0:T(8,128)(2,1)S(1)}, u32[]{:S(2)}) copy-start(bf16[96,3072]{1,0:T(8,128)(2,1)S(1)} %get-tuple-element.4) | copy-start | bytes 1769476
  414.1 28.7 %copy-start.1 = (bf16[3072,512]{1,0:T(8,128)(2,1)S(1)}, bf16[3072,512]{1,0:T(8,128)(2,1)}, u32[]{:S(2)}) copy-start(bf16[3072,512]{1,0:T(8,128)(2,1)} %param.20) | copy-start | bytes 9437188
Sparse Core Ops, SparseCore 0:
  194.2 151.6 all-reduce.3
  356.7 24.5 all-reduce.5
  414.2 26.1 all-reduce.7
where the time goes:
time: 450 us; the launch traced here: 449 us
  waiting for transfers between devices  203 us (45%)
  blocking collectives  155 us (34%)
  matrix products  51.7 us (11%)
  other arithmetic  19 us (4%)
  between operations  14.1 us (3%)
  local copies, waits for them, and re-layouts  6.17 us (1%)
    pmax x1, blocking collectives, local_step(): glob_max = lax.pmax(blk_max, 'sp')  155 us
    psum x1, waiting for transfers between devices, local_step(): lax.psum(jnp.concatenate([blk_mix * factor, blk_sum * factor], axis=-1),...  152 us
    psum x1, waiting for transfers between devices, local_step(): lax.psum(jnp.dot(act_prod, wd_loc, preferred_element_type=jnp.float32), '...  26.3 us
    psum x1, waiting for transfers between devices, local_step(): lax.psum(jnp.dot(attn_out, wo_loc, preferred_element_type=jnp.float32), '...  24.6 us
    dot_general x1, matrix products, local_step(): jnp.dot(act_prod, wd_loc, preferred_element_type=jnp.float32)  20.6 us
    dot_general x1, matrix products, local_step(): jnp.dot(h_norm, wg_loc, preferred_element_type=jnp.float32)  10.6 us
  transfers between devices with their start and end apart: 3, of which 3 were waited for; matrix products, arithmetic and copies ran while one was open for 0% of the time, Pallas kernels for 0%

commit v1 on v0

--- a/solution.py
+++ b/solution.py
@@ -1,10 +1,94 @@
 import jax
 import jax.numpy as jnp
 from jax import lax
+from jax.experimental import pallas as pl
+from jax.experimental.pallas import tpu as pltpu
 from jax.sharding import PartitionSpec as P
 
 ROPE_BASE = 500000.0
 NORM_EPS = 1e-5
+
+
+N_SP = 64
+N_OWN = 48
+MSG = 26
+
+def sp_id(t):
+    return {"sp": t}
+
+def combine_kernel(send_ref, out_ref, recv, mine, gath, fac, send_sem, recv_sem, gsend_sem, grecv_sem):
+    me = lax.axis_index("sp")
+    barrier = pltpu.get_barrier_semaphore()
+
+    @pl.loop(1, N_SP)
+    def _(j):
+        pl.semaphore_signal(barrier, inc=1, device_id=sp_id(lax.rem(me + j, N_SP)), device_id_type=pl.DeviceIdType.MESH)
+    pl.semaphore_wait(barrier, N_SP - 1)
+
+    @pl.loop(1, N_SP)
+    def _(j):
+        t = lax.rem(me + j, N_SP)
+        @pl.when(t < N_OWN)
+        def _():
+            pltpu.make_async_remote_copy(src_ref=send_ref.at[t], dst_ref=recv.at[me], send_sem=send_sem, recv_sem=recv_sem,
+                device_id=sp_id(t), device_id_type=pl.DeviceIdType.MESH).start()
+
+    @pl.when(me < N_OWN)
+    def _():
+        recv[me] = send_ref[me]
+        pltpu.make_async_copy(recv.at[pl.ds(0, N_SP - 1)], recv.at[pl.ds(0, N_SP - 1)], recv_sem).wait()
+        m = recv[:, 24, :]
+        l = recv[:, 25, :]
+        top = jnp.max(m, axis=0, keepdims=True)
+        f = jnp.exp(m - top)
+        tot = jnp.sum(f * l, axis=0, keepdims=True)
+        fac[...] = jnp.transpose(jnp.concatenate([f / tot, jnp.zeros((64, 128), jnp.float32)], axis=0))
+        base = pl.multiple_of(lax.div(me, 12) * 24, 8)
+        ft = fac[pl.ds(base, 24), :]
+        acc = jnp.zeros((24, 128), jnp.float32)
+        for i in range(N_SP):
+            acc = acc + recv[i, 0:24, :] * ft[:, i:i + 1]
+        mine[...] = acc.astype(jnp.bfloat16).astype(jnp.float32)
+        gath[me] = mine[...]
+
+        @pl.loop(1, N_SP)
+        def _(j):
+            t = lax.rem(me + j, N_SP)
+            pltpu.make_async_remote_copy(src_ref=mine, dst_ref=gath.at[me], send_sem=gsend_sem, recv_sem=grecv_sem,
+                device_id=sp_id(t), device_id_type=pl.DeviceIdType.MESH).start()
+        pltpu.make_async_copy(gath.at[pl.ds(0, N_OWN - 1)], gath.at[pl.ds(0, N_OWN - 1)], grecv_sem).wait()
+        pltpu.make_async_copy(send_ref.at[pl.ds(0, N_OWN - 1)], send_ref.at[pl.ds(0, N_OWN - 1)], send_sem).wait()
+        @pl.loop(1, N_SP)
+        def _(j):
+            pltpu.make_async_copy(mine, mine, gsend_sem).wait()
+
+    @pl.when(me >= N_OWN)
+    def _():
+        pltpu.make_async_copy(gath, gath, grecv_sem).wait()
+        pltpu.make_async_copy(send_ref, send_ref, send_sem).wait()
+
+    for kv in range(4):
+        for g in range(3):
+            h = kv * 3 + g
+            out_ref[:, h * 128:(h + 1) * 128] = gath[kv * 12:(kv + 1) * 12, g * 8:(g + 1) * 8, :].reshape(96, 128).astype(jnp.bfloat16)
+
+
+def combine(send):
+    return pl.pallas_call(
+        combine_kernel,
+        out_shape=jax.ShapeDtypeStruct((96, 1536), jnp.bfloat16),
+        in_specs=[pl.BlockSpec(memory_space=pltpu.VMEM)],
+        out_specs=pl.BlockSpec(memory_space=pltpu.VMEM),
+        scratch_shapes=[
+            pltpu.VMEM((N_SP, MSG, 128), jnp.float32),
+            pltpu.VMEM((24, 128), jnp.float32),
+            pltpu.VMEM((N_OWN, 24, 128), jnp.float32),
+            pltpu.VMEM((128, 128), jnp.float32),
+            pltpu.SemaphoreType.DMA, pltpu.SemaphoreType.DMA, pltpu.SemaphoreType.DMA, pltpu.SemaphoreType.DMA,
+        ],
+        compiler_params=pltpu.CompilerParams(collective_id=1, has_side_effects=True),
+        name="combine",
+    )(send)
 
 
 def rms_norm(x_in, norm_gain):
@@ -55,10 +139,14 @@
         weights = jnp.where(is_valid, jnp.exp(masked - blk_max), 0.0)
         blk_sum = jnp.sum(weights, axis=-1, keepdims=True)
         blk_mix = jnp.einsum("bkgs,bskd->bkgd", weights.astype(jnp.bfloat16), v_out, preferred_element_type=jnp.float32)
-        glob_max = lax.pmax(blk_max, "sp")
-        factor = jnp.exp(blk_max - glob_max)
-        packed = lax.psum(jnp.concatenate([blk_mix * factor, blk_sum * factor], axis=-1), "sp")
-        attn_out = (packed[..., :head_dim] / packed[..., head_dim:]).astype(jnp.bfloat16).reshape(batch_rows, q_loc * head_dim)
+        mix_rows = blk_mix.reshape(12, 8, kv_loc, groups, head_dim).transpose(2, 0, 3, 1, 4).reshape(48, 24, head_dim)
+
+        def stat_rows(stat):
+            lanes = stat.reshape(12, 8, kv_loc * groups).transpose(0, 2, 1).reshape(12, 1, 96)
+            return jnp.broadcast_to(jnp.pad(lanes, ((0, 0), (0, 0), (0, 32)))[None], (kv_loc, 12, 1, 128)).reshape(48, 1, 128)
+
+        send = jnp.concatenate([mix_rows, stat_rows(blk_max), stat_rows(blk_sum)], axis=1)
+        attn_out = combine(send)
         attn_proj = lax.psum(jnp.dot(attn_out, wo_loc, preferred_element_type=jnp.float32), "tp")
         hidden = (x_tok.astype(jnp.float32) + attn_proj).astype(jnp.bfloat16)
         h_norm = rms_norm(hidden, g_mlp)

time: 450 us -> 173 us (0.38)
  blocking collectives: 155 us -> 0 us
  waiting for transfers between devices: 203 us -> 50.8 us
  Pallas kernels: 0 us -> 33.5 us
    pmax x1 -> x0, blocking collectives: 155 us -> none  [local_step(): glob_max = lax.pmax(blk_max, 'sp')]
    psum x1 -> x0, waiting for transfers between devices: 152 us -> none  [local_step(): lax.psum(jnp.concatenate([blk_mix * factor, blk_sum * factor], axis=-1),...]
    pallas_call x0 -> x1, Pallas kernels: none -> 33.5 us  [combine(): pl.pallas_call(combine_kernel, out_shape=jax.ShapeDtypeStruct((96, 1536),...]
  transfers between devices with their start and end apart: 3 -> 2, of which waited for: 3 -> 2; matrix products, arithmetic and copies ran while one was open for 0% -> 0% of each run, Pallas kernels for 0% -> 0%
where the time goes in v1:
time: 173 us; the launch traced here: 172 us
  matrix products  52.5 us (30%)
  waiting for transfers between devices  50.8 us (29%)
  Pallas kernels  33.5 us (19%)
  other arithmetic  17.3 us (10%)
  between operations  14.3 us (8%)
  local copies, waits for them, and re-layouts  3.79 us (2%)
    pallas_call x1, Pallas kernels, combine(): pl.pallas_call(combine_kernel, out_shape=jax.ShapeDtypeStruct((96, 1536),...  33.5 us
    psum x1, waiting for transfers between devices, local_step(): lax.psum(jnp.dot(act_prod, wd_loc, preferred_element_type=jnp.float32), '...  26.3 us
    psum x1, waiting for transfers between devices, local_step(): lax.psum(jnp.dot(attn_out, wo_loc, preferred_element_type=jnp.float32), '...  24.5 us
    dot_general x1, matrix products, local_step(): jnp.dot(act_prod, wd_loc, preferred_element_type=jnp.float32)  20.7 us
    dot_general x1, matrix products, local_step(): jnp.dot(h_norm, wg_loc, preferred_element_type=jnp.float32)  10.6 us
    dot_general x1, matrix products, local_step(): jnp.dot(attn_out, wo_loc, preferred_element_type=jnp.float32)  6.44 us
    select_n x1, other arithmetic, local_step(): v_out = jnp.where(is_new, v_new[:, None], v_blk)  5.71 us
    dot_general x1, matrix products, local_step(): jnp.dot(x_norm, wq_loc, preferred_element_type=jnp.float32)  5.37 us
  transfers between devices with their start and end apart: 2, of which 2 were waited for; matrix products, arithmetic and copies ran while one was open for 0% of the time, Pallas kernels for 0%

profile of v1, /device:TPU:1, one launch (start us, length us, event | category | flops | bytes accessed | tf_op | source)
XLA Modules:
  0.0 172.5 jit_solution(9609142162714730628)
XLA Ops:
  7.2 0.0 copy-start
  7.2 0.0 all-reduce.5.cloned.1.call-start
  7.3 0.8 convert_element_type.85
  8.1 1.3 fusion.21
  9.4 0.7 convert_element_type.80
  10.1 0.7 broadcast_compare_fusion.1
  10.9 0.0 copy-done
  10.9 1.8 %convolution_convert_fusion.3 = bf16[96,512]{1,0:T(8,128)(2,1)S(1)} fusion(bf16[3072,512]{1,0:T(8,128)(2,1)S(1)} %copy-done, bf16[96,3072]{1,0:T(8,128)(2,1)} %param.13, f32[3072]{0:T(1024)S(1)} %convert_element_type.80, f32[96]{0:T(128)S(1)} %add_rsqrt_fusion.1), kind=kOutput, calls=%fused_computation.36 | convolution fusion | flops 303218688 | bytes 3846528 | tf_op jit(solution)/shard_map/dot_general | solution.py:127
  12.7 0.0 copy-start.2
  12.7 2.8 %fusion.29 = f32[96,512]{1,0:T(8,128)S(1)} fusion(bf16[3072,512]{1,0:T(8,128)(2,1)} %param.19, bf16[96,3072]{1,0:T(8,128)(2,1)} %param.13, f32[3072]{0:T(1024)S(1)} %convert_element_type.80, f32[96]{0:T(128)S(1)} %add_rsqrt_fusion.1), kind=kOutput, calls=%fused_computation.38 | convolution fusion | flops 303267840 | bytes 3944832 | tf_op jit(solution)/shard_map/dot_general | solution.py:126
  15.5 0.1 reshape.195
  15.6 0.0 copy-done.2
  15.6 5.4 %fusion.5 = f32[96,1536]{1,0:T(8,128)S(1)} fusion(bf16[3072,1536]{1,0:T(8,128)(2,1)} %param.18, bf16[96,3072]{1,0:T(8,128)(2,1)S(1)} %copy-done.2, f32[3072]{0:T(1024)S(1)} %convert_element_type.80, f32[96]{0:T(128)S(1)} %add_rsqrt_fusion.1), kind=kOutput, calls=%fused_computation.8 | convolution fusion | flops 907444224 | bytes 10629504 | tf_op jit(solution)/shard_map/dot_general | solution.py:125
  21.0 0.1 reshape.194
  21.1 0.2 multiply_cosine_fusion
  21.3 0.2 subtract_convert_fusion.1
  21.6 0.4 subtract_convert_fusion
  21.9 0.3 copy.34
  22.2 0.3 copy.36
  22.6 0.3 copy.35
  22.9 0.3 copy.37
  23.3 0.1 pad_maximum_fusion.1
  23.4 5.7 %broadcast_select_fusion = (bf16[96,16,4,128]{3,2,1,0:T(4,128)(2,1)S(1)}, bf16[96,16,4,128]{3,2,1,0:T(4,128)(2,1)S(1)}) fusion(bf16[96,16,4,128]{3,2,1,0:T(4,128)(2,1)} %param.16, pred[96,16]{1,0:T(8,128)(4,1)S(1)} %get-tuple-element.12, bf16[96,4,128]{2,1,0:T(4,128)(2,1)S(1)} %broadcast_in_dim.85, bf16[96,16,4,128]{3,2,1,0:T(4,128)(2,1)} %param.15, ...), kind=kLoop, calls=%fused_computation.24 | loop fusion | flops 1572864 | bytes 6489600 | tf_op jit(solution)/shard_map/jit(_where)/select_n | solution.py:133
  29.1 0.0 copy-start.5
  29.1 0.0 copy-start.4
  29.1 2.1 %fusion.50 = (f32[96,4,3]{2,1,0:T(4,128)S(1)}, f32[96,4,3,16]{3,2,1,0:T(4,128)}) fusion(bf16[96,16,4,128]{3,2,1,0:T(4,128)(2,1)S(1)} %get-tuple-element.10, bf16[96,4,3,64]{3,2,1,0:T(4,128)(2,1)S(1)} %copy.37, bf16[96,4,3,64]{3,2,1,0:T(4,128)(2,1)S(1)} %copy.36, pred[96,16]{1,0:T(8,128)(4,1)S(1)} %get-tuple-element.11), kind=kOutput, calls=%fused_computation.68 | convolution fusion | flops 5362560 | bytes 1947648 | tf_op jit(solution)/shard_map/bkgd,bskd->bkgs/dot_general | solution.py:135
  31.3 0.0 copy-done.5
  31.3 0.1 copy.41
  31.4 0.1 reshape_broadcast_in_dim.6
  31.5 0.1 copy.42
  31.7 0.1 copy.43
  31.8 2.1 %fusion.31 = f32[96,4,3]{2,1,0:T(4,128)S(1)} fusion(f32[96,4,3,16]{3,2,1,0:T(4,128)} %get-tuple-element.16, f32[96,4,3]{2,1,0:T(4,128)S(1)} %get-tuple-element.15, pred[96,16]{1,0:T(8,128)(4,1)S(1)} %get-tuple-element.11), kind=kLoop, calls=%fused_computation.44 | loop fusion | flops 54144 | bytes 84480 | tf_op jit(solution)/shard_map/reduce_sum | solution.py:140
  33.9 0.0 copy-done.4
  33.9 2.7 %fusion.6 = f32[96,4,3,128]{3,2,1,0:T(4,128)} fusion(bf16[96,16,4,128]{3,2,1,0:T(4,128)(2,1)S(1)} %get-tuple-element.9, f32[96,4,3,16]{3,2,1,0:T(4,128)} %get-tuple-element.16, f32[96,4,3]{2,1,0:T(4,128)S(1)} %get-tuple-element.15, pred[96,16]{1,0:T(8,128)(4,1)S(1)} %get-tuple-element.11), kind=kOutput, calls=%fused_computation.15 | convolution fusion | flops 4773888 | bytes 2242560 | tf_op jit(solution)/shard_map/bkgs,bskd->bkgd/dot_general | solution.py:141
  36.6 0.1 copy.44
  36.7 1.4 copy.40
  38.1 0.1 reshape_broadcast_in_dim.7
  38.2 0.1 copy.45
  38.3 0.1 copy.46
  38.4 1.0 pad_maximum_fusion.send_ref
  39.4 33.5 %combine.1 = bf16[96,1536]{1,0:T(8,128)(2,1)} custom-call(f32[48,26,128]{2,1,0:T(8,128)} %pad_maximum_fusion.send_ref), custom_call_target="tpu_custom_call" | custom-call | tf_op jit(solution)/shard_map/combine/pallas_call | solution.py:77
  72.9 0.0 copy-start.6
  72.9 6.4 %fusion.51 = f32[96,3072]{1,0:T(8,128)} fusion(bf16[96,1536]{1,0:T(8,128)(2,1)} %combine.1, bf16[1536,3072]{1,0:T(8,128)(2,1)} %param.21), kind=kOutput, calls=%fused_computation.69 | convolution fusion | flops 905969664 | bytes 10911744 | tf_op jit(solution)/shard_map/dot_general | solution.py:150
  79.4 0.0 all-reduce.5.cloned.1.call-update
  79.4 0.2 all-reduce.7.cloned.1.call-start
  79.6 0.0 copy-done.6
  79.6 24.5 %all-reduce.5.cloned.1.call-done = f32[96,3072]{1,0:T(8,128)} async-done(((f32[96,3072]{1,0:T(8,128)}), f32[96,3072]{1,0:T(8,128)}) %all-reduce.5.cloned.1.call-update) | async-done | bytes 1179664 | tf_op jit(solution)/shard_map/psum | solution.py:150
  104.1 1.5 fusion.25
  105.7 0.0 copy-start.3
  105.7 10.6 %fusion.3 = f32[96,4096]{1,0:T(8,128)S(1)} fusion(bf16[3072,4096]{1,0:T(8,128)(2,1)} %param.23, bf16[96,3072]{1,0:T(8,128)(2,1)S(1)} %get-tuple-element.4, f32[3072]{0:T(1024)S(1)} %convert_element_type.93, f32[96]{0:T(128)S(1)} %add_rsqrt_fusion), kind=kOutput, calls=%fused_computation.5 | convolution fusion | flops 2417885184 | bytes 27341184 | tf_op jit(solution)/shard_map/dot_general | solution.py:153
  116.3 0.0 copy-done.3
  116.3 20.7 %fusion.4 = f32[96,3072]{1,0:T(8,128)} fusion(bf16[4096,3072]{1,0:T(8,128)(2,1)} %param.25, bf16[3072,4096]{1,0:T(8,128)(2,1)} %param.24, f32[96,4096]{1,0:T(8,128)S(1)} %fusion.3, bf16[96,3072]{1,0:T(8,128)(2,1)S(1)} %get-tuple-element.4, f32[3072]{0:T(1024)S(1)} %convert_element_type.93, f32[96]{0:T(128)S(1)} %add_rsqrt_fusion), kind=kOutput, calls=%fused_computation.6 | convolution fusion | flops 4836163584 | bytes 53686656 | tf_op jit(solution)/shard_map/dot_general | solution.py:156
  137.0 0.0 copy-start.1
  137.0 0.0 all-reduce.7.cloned.1.call-update
  137.0 26.3 %all-reduce.7.cloned.1.call-done = f32[96,3072]{1,0:T(8,128)} async-done(((f32[96,3072]{1,0:T(8,128)}), f32[96,3072]{1,0:T(8,128)}) %all-reduce.7.cloned.1.call-update) | async-done | bytes 1179664 | tf_op jit(solution)/shard_map/psum | solution.py:156
  163.3 2.3 %fusion.28 = bf16[96,3072]{1,0:T(8,128)(2,1)} fusion(f32[96,3072]{1,0:T(8,128)} %all-reduce.7.cloned.1.call-done, bf16[96,3072]{1,0:T(8,128)(2,1)} %copy-done.3), kind=kLoop, calls=%fused_computation.35 | loop fusion | flops 884736 | bytes 2359296 | tf_op jit(solution)/shard_map/convert_element_type | solution.py:157
  165.6 0.0 copy-done.1
  (12 shorter events, 0.1 us)
Async XLA Ops:
  7.2 3.7 %copy-start = (bf16[3072,512]{1,0:T(8,128)(2,1)S(1)}, bf16[3072,512]{1,0:T(8,128)(2,1)}, u32[]{:S(2)}) copy-start(bf16[3072,512]{1,0:T(8,128)(2,1)} %param.20) | copy-start | bytes 9437188
  7.2 96.9 %all-reduce.5.cloned.1.call-start = ((), (), s32[]{:S(2)}) async-start(), calls=%async_computation | async-start | bytes 2359296 | tf_op jit(solution)/shard_map/psum | solution.py:150
  12.7 2.9 %copy-start.2 = (bf16[96,3072]{1,0:T(8,128)(2,1)S(1)}, bf16[96,3072]{1,0:T(8,128)(2,1)}, u32[]{:S(2)}) copy-start(bf16[96,3072]{1,0:T(8,128)(2,1)} %param.13) | copy-start | bytes 1769476
  29.1 2.2 %copy-start.5 = (bf16[96,16,4,128]{3,2,1,0:T(4,128)(2,1)}, bf16[96,16,4,128]{3,2,1,0:T(4,128)(2,1)S(1)}, u32[]{:S(2)}) copy-start(bf16[96,16,4,128]{3,2,1,0:T(4,128)(2,1)S(1)} %get-tuple-element.10) | copy-start | bytes 4718596
  29.1 4.7 %copy-start.4 = (bf16[96,16,4,128]{3,2,1,0:T(4,128)(2,1)}, bf16[96,16,4,128]{3,2,1,0:T(4,128)(2,1)S(1)}, u32[]{:S(2)}) copy-start(bf16[96,16,4,128]{3,2,1,0:T(4,128)(2,1)S(1)} %get-tuple-element.9) | copy-start | bytes 4718596
  72.9 6.7 %copy-start.6 = (bf16[3072]{0:T(1024)(128)(2,1)S(1)}, bf16[3072]{0:T(1024)(128)(2,1)}, u32[]{:S(2)}) copy-start(bf16[3072]{0:T(1024)(128)(2,1)} %param.22) | copy-start | bytes 18436
  79.4 83.9 %all-reduce.7.cloned.1.call-start = ((), (), s32[]{:S(2)}) async-start(), calls=%async_computation.1 | async-start | bytes 2359296 | tf_op jit(solution)/shard_map/psum | solution.py:156
  105.7 10.6 %copy-start.3 = (bf16[96,3072]{1,0:T(8,128)(2,1)}, bf16[96,3072]{1,0:T(8,128)(2,1)S(1)}, u32[]{:S(2)}) copy-start(bf16[96,3072]{1,0:T(8,128)(2,1)S(1)} %get-tuple-element.4) | copy-start | bytes 1769476
  137.0 28.7 %copy-start.1 = (bf16[3072,512]{1,0:T(8,128)(2,1)S(1)}, bf16[3072,512]{1,0:T(8,128)(2,1)}, u32[]{:S(2)}) copy-start(bf16[3072,512]{1,0:T(8,128)(2,1)} %param.20) | copy-start | bytes 9437188
Sparse Core Ops, SparseCore 0:
  79.5 24.5 all-reduce.4
  137.1 26.1 all-reduce.6

commit v2 on v0

v2 whole, which is shorter than its diff:
```python
import jax
import jax.numpy as jnp
from jax import lax
from jax.experimental import pallas as pl
from jax.experimental.pallas import tpu as pltpu
from jax.sharding import PartitionSpec as P

ROPE_BASE = 500000.0
NORM_EPS = 1e-5
N_SP = 64
N_OWN = 48
MSG = 26
SLOTS = 16
MESH = pl.DeviceIdType.MESH


def rest_kernel(send_ref, x_ref, g_ref, wo, wg, wu, wd, y_ref,
                recv, mine, gath, fac, attn, part, prem, hid, z_scr, act, wbuf,
                send_sem, recv_sem, gsend_sem, grecv_sem, psend_sem, precv_sem, wsem):
    me = lax.axis_index("sp")
    tp = lax.axis_index("tp")
    barrier = pltpu.get_barrier_semaphore()

    @pl.loop(1, N_SP)
    def _(j):
        pl.semaphore_signal(barrier, inc=1, device_id={"sp": lax.rem(me + j, N_SP)}, device_id_type=MESH)
    pl.semaphore_signal(barrier, inc=1, device_id={"tp": 1 - tp}, device_id_type=MESH)

    def cols(c):
        return pl.ds(pl.multiple_of(c * 512, 512), 512)

    def load(src, slot, rows):
        return pltpu.make_async_copy(src, wbuf.at[slot, rows], wsem.at[slot])

    def start_wo(j):
        for half in range(2):
            load(wo.at[:, pl.ds((2 * j + half) * 512, 512)], j, pl.ds(half * 1536, 1536)).start()

    def start_gu(c):
        load(wg.at[:, cols(c)], lax.rem(3 + 2 * c, SLOTS), pl.ds(0, 3072)).start()
        load(wu.at[:, cols(c)], lax.rem(4 + 2 * c, SLOTS), pl.ds(0, 3072)).start()

    def start_wd(m):
        for third in range(3):
            piece = 3 * m + third
            n, kq = lax.div(piece, 4), lax.rem(piece, 4)
            load(wd.at[pl.ds(pl.multiple_of(kq * 1024, 1024), 1024), cols(n)], lax.rem(3 + m, SLOTS), pl.ds(third * 1024, 1024)).start()

    def arrived(slot):
        pltpu.make_async_copy(wbuf.at[slot], wbuf.at[slot], wsem.at[slot]).wait()

    for j in range(3):
        start_wo(j)

    @pl.loop(0, 6)
    def _(c):
        start_gu(c)
    load(wg.at[:, pl.ds(6 * 512, 512)], 15, pl.ds(0, 3072)).start()

    pl.semaphore_wait(barrier, N_SP)

    @pl.loop(1, N_SP)
    def _(j):
        t = lax.rem(me + j, N_SP)

        @pl.when(t < N_OWN)
        def _():
            pltpu.make_async_remote_copy(src_ref=send_ref.at[t], dst_ref=recv.at[me], send_sem=send_sem, recv_sem=recv_sem,
                                         device_id={"sp": t}, device_id_type=MESH).start()

    @pl.when(me < N_OWN)
    def _():
        recv[me] = send_ref[me]
        pltpu.make_async_copy(recv.at[pl.ds(0, N_SP - 1)], recv.at[pl.ds(0, N_SP - 1)], recv_sem).wait()
        top = jnp.max(recv[:, 24, :], axis=0, keepdims=True)
        f = jnp.exp(recv[:, 24, :] - top)
        tot = jnp.sum(f * recv[:, 25, :], axis=0, keepdims=True)
        fac[...] = jnp.transpose(jnp.concatenate([f, jnp.broadcast_to(tot, (64, 128))], axis=0))
        ft = fac[pl.ds(pl.multiple_of(lax.div(me, 12) * 24, 8), 24), :]
        acc = [jnp.zeros((24, 128), jnp.float32) for _ in range(4)]
        for i in range(N_SP):
            acc[i % 4] = acc[i % 4] + recv[i, 0:24, :] * ft[:, i:i + 1]
        total = (acc[0] + acc[1]) + (acc[2] + acc[3])
        mine[...] = (total / ft[:, 64:65]).astype(jnp.bfloat16).astype(jnp.float32)
        gath[me] = mine[...]

        @pl.loop(1, N_SP)
        def _(j):
            pltpu.make_async_remote_copy(src_ref=mine, dst_ref=gath.at[me], send_sem=gsend_sem, recv_sem=grecv_sem,
                                         device_id={"sp": lax.rem(me + j, N_SP)}, device_id_type=MESH).start()
        pltpu.make_async_copy(gath.at[pl.ds(0, N_OWN - 1)], gath.at[pl.ds(0, N_OWN - 1)], grecv_sem).wait()

    @pl.when(me >= N_OWN)
    def _():
        pltpu.make_async_copy(gath, gath, grecv_sem).wait()

    for kv in range(4):
        for g in range(3):
            h = kv * 3 + g
            attn[:, h * 128:(h + 1) * 128] = gath[kv * 12:(kv + 1) * 12, g * 8:(g + 1) * 8, :].reshape(96, 128).astype(jnp.bfloat16)

    def exchange(phase, n):
        return pltpu.make_async_remote_copy(src_ref=part.at[phase, n], dst_ref=prem.at[phase, n], send_sem=psend_sem.at[phase, n],
                                            recv_sem=precv_sem.at[phase, n], device_id={"tp": 1 - tp}, device_id_type=MESH)

    for j in range(3):
        arrived(j)
        for half in range(2):
            n = 2 * j + half
            part[0, n] = jnp.dot(attn[...], wbuf[j, half * 1536:(half + 1) * 1536, :], preferred_element_type=jnp.float32)
            exchange(0, n).start()
        if j == 0:
            load(wu.at[:, pl.ds(6 * 512, 512)], 0, pl.ds(0, 3072)).start()
        if j == 1:
            load(wg.at[:, pl.ds(7 * 512, 512)], 1, pl.ds(0, 3072)).start()
        if j == 2:
            load(wu.at[:, pl.ds(7 * 512, 512)], 2, pl.ds(0, 3072)).start()
    sq = jnp.zeros((96, 128), jnp.float32)
    for n in range(6):
        exchange(0, n).wait_recv()
        for q in range(4):
            at = slice(n * 512 + q * 128, n * 512 + (q + 1) * 128)
            here = slice(q * 128, (q + 1) * 128)
            h = (x_ref[:, at].astype(jnp.float32) + (part[0, n, :, here] + prem[0, n, :, here])).astype(jnp.bfloat16)
            hid[:, at] = h
            h = h.astype(jnp.float32)
            sq = sq + h * h
    inv = lax.rsqrt(jnp.sum(sq, axis=-1, keepdims=True) * (1.0 / 3072.0) + NORM_EPS)
    for c in range(24):
        at = slice(c * 128, (c + 1) * 128)
        z_scr[:, at] = (hid[:, at].astype(jnp.float32) * inv * g_ref[c:c + 1, :].astype(jnp.float32)).astype(jnp.bfloat16)

    @pl.loop(0, 8)
    def _(c):
        sg = lax.rem(3 + 2 * c, SLOTS)
        su = lax.rem(4 + 2 * c, SLOTS)
        arrived(sg)
        gate = jnp.dot(z_scr[...], wbuf[sg], preferred_element_type=jnp.float32).astype(jnp.bfloat16).astype(jnp.float32)
        arrived(su)
        up = jnp.dot(z_scr[...], wbuf[su], preferred_element_type=jnp.float32).astype(jnp.bfloat16).astype(jnp.float32)
        act[:, cols(c)] = (gate * lax.logistic(gate) * up).astype(jnp.bfloat16)

        @pl.when(c < 4)
        def _():
            start_wd(2 * c)
            start_wd(2 * c + 1)

    waited = -1
    for n in range(6):
        total = None
        for kq in range(4):
            m, third = divmod(n * 4 + kq, 3)
            if m > waited:
                arrived((3 + m) % SLOTS)
                waited = m
            d = jnp.dot(act[:, kq * 1024:(kq + 1) * 1024], wbuf[(3 + m) % SLOTS, third * 1024:(third + 1) * 1024, :], preferred_element_type=jnp.float32)
            total = d if total is None else total + d
        part[1, n] = total
        exchange(1, n).start()
    for n in range(6):
        exchange(1, n).wait_recv()
        at = slice(n * 512, (n + 1) * 512)
        y_ref[:, at] = (hid[:, at].astype(jnp.float32) + (part[1, n] + prem[1, n])).astype(jnp.bfloat16)

    for n in range(6):
        exchange(0, n).wait_send()
        exchange(1, n).wait_send()

    @pl.when(me < N_OWN)
    def _():
        pltpu.make_async_copy(send_ref.at[pl.ds(0, N_OWN - 1)], send_ref.at[pl.ds(0, N_OWN - 1)], send_sem).wait()

        @pl.loop(1, N_SP)
        def _(j):
            pltpu.make_async_copy(mine, mine, gsend_sem).wait()

    @pl.when(me >= N_OWN)
    def _():
        pltpu.make_async_copy(send_ref, send_ref, send_sem).wait()


def rest_part(send, x_tok, g_mlp, wo, wg, wu, wd):
    vmem = pl.BlockSpec(memory_space=pltpu.VMEM)
    hbm = pl.BlockSpec(memory_space=pl.ANY)
    f32, bf16 = jnp.float32, jnp.bfloat16
    return pl.pallas_call(
        rest_kernel,
        out_shape=jax.ShapeDtypeStruct((96, 3072), bf16),
        in_specs=[vmem, vmem, vmem, hbm, hbm, hbm, hbm],
        out_specs=vmem,
        scratch_shapes=[
            pltpu.VMEM((N_SP, MSG, 128), f32),
            pltpu.VMEM((24, 128), f32),
            pltpu.VMEM((N_OWN, 24, 128), f32),
            pltpu.VMEM((128, 128), f32),
            pltpu.VMEM((96, 1536), bf16),
            pltpu.VMEM((2, 6, 96, 512), f32),
            pltpu.VMEM((2, 6, 96, 512), f32),
            pltpu.VMEM((96, 3072), bf16),
            pltpu.VMEM((96, 3072), bf16),
            pltpu.VMEM((96, 4096), bf16),
            pltpu.VMEM((SLOTS, 3072, 512), bf16),
            pltpu.SemaphoreType.DMA, pltpu.SemaphoreType.DMA, pltpu.SemaphoreType.DMA, pltpu.SemaphoreType.DMA,
            pltpu.SemaphoreType.DMA((2, 6)), pltpu.SemaphoreType.DMA((2, 6)), pltpu.SemaphoreType.DMA((SLOTS,)),
        ],
        compiler_params=pltpu.CompilerParams(collective_id=1, has_side_effects=True, vmem_limit_bytes=67043328),
        cost_estimate=pl.CostEstimate(flops=2 * 96 * 42_500_000, bytes_accessed=90_000_000, transcendentals=400_000),
        name="rest_part",
    )(send, x_tok, g_mlp.reshape(24, 128), wo, wg, wu, wd)


def local_kernel(seq_ref, x_ref, g_ref, cos_ref, sin_ref, kin, vin, wq, wk, wv,
                 send_ref, kout, vout, wbuf, kbuf, vbuf, u_scr, q_scr, new_scr, wsem, csem, osem):
    sp = lax.axis_index("sp")
    chunks = [(wk, 0), (wv, 0), (wq, 0), (wq, 1), (wq, 2)]
    wcopies = [pltpu.make_async_copy(w.at[:, pl.ds(c * 512, 512)], wbuf.at[i], wsem.at[i]) for i, (w, c) in enumerate(chunks)]
    kcopy = pltpu.make_async_copy(kin, kbuf, csem.at[0])
    vcopy = pltpu.make_async_copy(vin, vbuf, csem.at[1])
    for copy in wcopies[:2] + [kcopy, vcopy] + wcopies[2:]:
        copy.start()

    sq = jnp.zeros((96, 128), jnp.float32)
    for c in range(24):
        xc = x_ref[:, c * 128:(c + 1) * 128].astype(jnp.float32)
        sq = sq + xc * xc
    inv = lax.rsqrt(jnp.sum(sq, axis=-1, keepdims=True) * (1.0 / 3072.0) + NORM_EPS)
    for c in range(24):
        xc = x_ref[:, c * 128:(c + 1) * 128].astype(jnp.float32)
        u_scr[:, c * 128:(c + 1) * 128] = (xc * inv * g_ref[c:c + 1, :].astype(jnp.float32)).astype(jnp.bfloat16)
    u = u_scr[...]
    cos_a = cos_ref[...]
    sin_a = sin_ref[...]

    def project(i):
        wcopies[i].wait()
        return jnp.dot(u, wbuf[i], preferred_element_type=jnp.float32).astype(jnp.bfloat16).astype(jnp.float32)

    def rope(h):
        return (h * cos_a + pltpu.roll(h, 64, 1) * sin_a).astype(jnp.bfloat16).astype(jnp.float32)

    rowpos = lax.broadcasted_iota(jnp.int32, (64, 128), 0) // 4 + sp * 16

    def update(i, cin, buf, turn, out, sem):
        fresh = project(i)
        for kv in range(4):
            rows = fresh[:, kv * 128:(kv + 1) * 128]
            rows = rope(rows) if turn else rows
            new_scr[pl.ds(kv, 96, stride=8), :] = rows
            new_scr[pl.ds(kv + 4, 96, stride=8), :] = rows
        cin.wait()

        @pl.loop(0, 12)
        def _(bg):
            for j in range(8):
                b = bg * 8 + j
                tile = new_scr[pl.ds(pl.multiple_of(b * 8, 8), 8), :]
                old = buf[b].astype(jnp.float32)
                wide = jnp.broadcast_to(tile[None], (8, 8, 128)).reshape(64, 128)
                buf[b] = jnp.where(rowpos == seq_ref[b], wide, old).astype(jnp.bfloat16)
        copy = pltpu.make_async_copy(buf, out, sem)
        copy.start()
        return copy

    ocopies = [update(0, kcopy, kbuf, True, kout, osem.at[0]), update(1, vcopy, vbuf, False, vout, osem.at[1])]

    for c in range(3):
        q = project(2 + c)
        for j in range(4):
            q_scr[:, c * 4 + j] = rope(q[:, j * 128:(j + 1) * 128]).reshape(12, 8, 128)

    col = lax.broadcasted_iota(jnp.int32, (8, 512), 1)
    sub = lax.broadcasted_iota(jnp.int32, (8, 512), 0)
    own_req = (col // 64) == sub
    colpos = (col % 64) // 4 + sp * 16
    diag = lax.broadcasted_iota(jnp.int32, (96, 128), 0) == lax.broadcasted_iota(jnp.int32, (96, 128), 1)

    @pl.loop(0, 12)
    def _(bg):
        q = q_scr[bg].reshape(96, 128).astype(jnp.bfloat16)
        k = kbuf[pl.ds(bg * 8, 8)].reshape(512, 128)
        v = vbuf[pl.ds(bg * 8, 8)].reshape(512, 128)
        s = lax.dot_general(q, k, (((1,), (1,)), ((), ())), preferred_element_type=jnp.float32) * (128.0 ** -0.5)
        last = jnp.zeros((8, 512), jnp.int32)
        for j in range(8):
            last = jnp.where(sub == j, seq_ref[bg * 8 + j], last)
        ok = own_req & (colpos <= last)
        weights, tops, sums = [], [], []
        for kv in range(4):
            seen = ok & ((col % 4) == kv)
            for g in range(3):
                h = kv * 3 + g
                masked = jnp.where(seen, s[h * 8:(h + 1) * 8, :], -1e30)
                top = jnp.max(masked, axis=-1, keepdims=True)
                w = jnp.where(seen, jnp.exp(masked - top), 0.0)
                weights.append(w)
                tops.append(jnp.broadcast_to(top, (8, 128)))
                sums.append(jnp.broadcast_to(jnp.sum(w, axis=-1, keepdims=True), (8, 128)))
        w = jnp.concatenate(weights, axis=0).astype(jnp.bfloat16)
        mix = jnp.dot(w, v, preferred_element_type=jnp.float32)
        top_row = jnp.sum(jnp.where(diag, jnp.concatenate(tops, axis=0), 0.0), axis=0, keepdims=True)
        sum_row = jnp.sum(jnp.where(diag, jnp.concatenate(sums, axis=0), 0.0), axis=0, keepdims=True)
        for kv in range(4):
            send_ref[kv * 12 + bg, 0:24, :] = mix[kv * 24:(kv + 1) * 24, :]
            send_ref[kv * 12 + bg, 24:25, :] = top_row
            send_ref[kv * 12 + bg, 25:26, :] = sum_row

    for copy in ocopies:
        copy.wait()


def local_part(seq_lens, x_tok, g_attn, k_blk, v_blk, wq, wk, wv):
    inv_freq = jnp.power(jnp.float32(ROPE_BASE), jnp.arange(64, dtype=jnp.float32) * (-2.0 / 128))
    angles = seq_lens.astype(jnp.float32)[:, None] * inv_freq
    cos_a, sin_a = jnp.cos(angles), jnp.sin(angles)
    cos2 = jnp.concatenate([cos_a, cos_a], axis=-1)
    sin2 = jnp.concatenate([-sin_a, sin_a], axis=-1)
    vmem = pl.BlockSpec(memory_space=pltpu.VMEM)
    hbm = pl.BlockSpec(memory_space=pl.ANY)
    cache = jax.ShapeDtypeStruct((96, 64, 128), jnp.bfloat16)
    send, k_out, v_out = pl.pallas_call(
        local_kernel,
        out_shape=(jax.ShapeDtypeStruct((48, MSG, 128), jnp.float32), cache, cache),
        in_specs=[pl.BlockSpec(memory_space=pltpu.SMEM), vmem, vmem, vmem, vmem, hbm, hbm, hbm, hbm, hbm],
        out_specs=(vmem, hbm, hbm),
        scratch_shapes=[
            pltpu.VMEM((5, 3072, 512), jnp.bfloat16),
            pltpu.VMEM((96, 64, 128), jnp.bfloat16),
            pltpu.VMEM((96, 64, 128), jnp.bfloat16),
            pltpu.VMEM((96, 3072), jnp.bfloat16),
            pltpu.VMEM((12, 12, 8, 128), jnp.float32),
            pltpu.VMEM((768, 128), jnp.float32),
            pltpu.SemaphoreType.DMA((5,)),
            pltpu.SemaphoreType.DMA((2,)),
            pltpu.SemaphoreType.DMA((2,)),
        ],
        compiler_params=pltpu.CompilerParams(vmem_limit_bytes=67043328),
        cost_estimate=pl.CostEstimate(flops=2 * 96 * 3072 * 2560, bytes_accessed=22_000_000, transcendentals=600_000),
        name="local_part",
    )(seq_lens, x_tok, g_attn.reshape(24, 128), cos2, sin2, k_blk.reshape(96, 64, 128), v_blk.reshape(96, 64, 128), wq, wk, wv)
    return send, k_out.reshape(k_blk.shape), v_out.reshape(v_blk.shape)


def solution(mesh):
    cache_spec = P(None, "sp", "tp", None)
    col_spec = P(None, "tp")
    row_spec = P("tp", None)
    full_spec = P()

    def local_step(x_tok, seq_lens, k_blk, v_blk, g_attn, wq_loc, wk_loc, wv_loc, wo_loc, g_mlp, wg_loc, wu_loc, wd_loc):
        send, k_out, v_out = local_part(seq_lens, x_tok, g_attn, k_blk, v_blk, wq_loc, wk_loc, wv_loc)
        y_out = rest_part(send, x_tok, g_mlp, wo_loc, wg_loc, wu_loc, wd_loc)
        return y_out, k_out, v_out

    return jax.shard_map(local_step, mesh=mesh, in_specs=(full_spec, full_spec, cache_spec, cache_spec, full_spec, col_spec, col_spec, col_spec, row_spec, full_spec, col_spec, col_spec, row_spec), out_specs=(full_spec, cache_spec, cache_spec), check_vma=False)
```

time: 450 us -> 75.8 us (0.17)
  waiting for transfers between devices: 203 us -> 0 us
  blocking collectives: 155 us -> 0 us
  Pallas kernels: 0 us -> 71.4 us
  matrix products: 51.7 us -> 0 us
  other arithmetic: 19 us -> 1.66 us
  between operations: 14.1 us -> 0.65 us
    psum x3 -> x0, waiting for transfers between devices: 203 us -> none  [the longest x1 152 us: local_step(): lax.psum(jnp.concatenate([blk_mix * factor, blk_sum * factor], axis=-1),...]
    pmax x1 -> x0, blocking collectives: 155 us -> none  [local_step(): glob_max = lax.pmax(blk_max, 'sp')]
    pallas_call x0 -> x2, Pallas kernels: none -> 71.4 us  [the longest x1 56.3 us: rest_part(): pl.pallas_call(rest_kernel, out_shape=jax.ShapeDtypeStruct((96, 3072), bf...]
    dot_general x8 -> x0, matrix products: 51.7 us -> none  [the longest x1 20.6 us: local_step(): jnp.dot(act_prod, wd_loc, preferred_element_type=jnp.float32)]
    select_n x1 -> x0, other arithmetic: 5.71 us -> none  [local_step(): v_out = jnp.where(is_new, v_new[:, None], v_blk)]
    reduce_sum x3 -> x0, other arithmetic: 4.97 us -> none  [the longest x2 2.88 us: rms_norm(): jnp.mean(x_f32 * x_f32, axis=-1, keepdims=True) + NORM_EPS]
  transfers between devices with their start and end apart: 3 -> 0, of which waited for: 3 -> 0; matrix products, arithmetic and copies ran while one was open for 0% -> 0% of each run, Pallas kernels for 0% -> 0%
where the time goes in v2:
time: 75.8 us; the launch traced here: 75.6 us
  Pallas kernels  71.4 us (94%)
  local copies, waits for them, and re-layouts  1.92 us (3%)
  other arithmetic  1.66 us (2%)
    pallas_call x1, Pallas kernels, rest_part(): pl.pallas_call(rest_kernel, out_shape=jax.ShapeDtypeStruct((96, 3072), bf...  56.3 us
    pallas_call x1, Pallas kernels, local_part(): pl.pallas_call(local_kernel, out_shape=(jax.ShapeDtypeStruct((48, MSG, 12...  15.1 us
    unnamed x1, local copies, waits for them, and re-layouts  1.92 us

profile of v2, /device:TPU:1, one launch (start us, length us, event | category | flops | bytes accessed | tf_op | source)
XLA Modules:
  0.0 75.6 jit_solution(7070437388019269581)
XLA Ops:
  0.6 0.7 convert_element_type.3
  1.3 0.3 fusion
  1.6 0.7 pad_maximum_fusion
  2.3 15.1 %local_part.1 = (f32[48,26,128]{2,1,0:T(8,128)}, bf16[96,64,128]{2,1,0:T(8,128)(2,1)}, bf16[96,64,128]{2,1,0:T(8,128)(2,1)}) custom-call(s32[96]{0:T(128)} %seq_ref.1, bf16[96,3072]{1,0:T(8,128)(2,1)} %x_ref.3, bf16[24,128]{1,0:T(8,128)(2,1)} %bitcast.9, f32[96,128]{1,0:T(8,128)} %get-tuple-element.12.cos_ref, f32[96,128]{1,0:T(8,128)} %get-tuple-element.13.sin_ref, ...), custom_call_target="tpu_custom_call" | custom-call | flops 1509949440 | bytes 22000000 | tf_op jit(solution)/shard_map/local_part/pallas_call | solution.py:320
  17.4 56.3 %rest_part.1 = bf16[96,3072]{1,0:T(8,128)(2,1)} custom-call(f32[48,26,128]{2,1,0:T(8,128)} %get-tuple-element.6.send_ref, bf16[96,3072]{1,0:T(8,128)(2,1)} %x_ref.3, bf16[24,128]{1,0:T(8,128)(2,1)} %bitcast.8, bf16[1536,3072]{1,0:T(8,128)(2,1)} %wo.1, bf16[3072,4096]{1,0:T(8,128)(2,1)} %wg.1, bf16[3072,4096]{1,0:T(8,128)(2,1)} %wu.1, bf16[4096,3072]{1,0:T(8,128)(2,1)} %wd.1), custom_call_target="tpu_custom_call" | custom-call | flops 8160000000 | bytes 90000000 | tf_op jit(solution)/shard_map/rest_part/pallas_call | solution.py:186
  73.7 1.9 %copy.17 = bf16[96,3072]{1,0:T(8,128)(2,1)} copy(bf16[96,3072]{1,0:T(8,128)(2,1)} %rest_part.1) | data formatting | bytes 1179648
  (1 shorter events, 0.0 us)

commit v3 on v0

v3 whole, which is shorter than its diff:
```python
import jax
import jax.numpy as jnp
import numpy as np
from jax import lax
from jax.experimental import pallas as pl
from jax.experimental.pallas import tpu as pltpu
from jax.sharding import PartitionSpec as P

ROPE_BASE = 500000.0
NORM_EPS = 1e-5
N_SP = 64
N_OWN = 48
MSG = 26
SLOTS = 16
MESH = pl.DeviceIdType.MESH


def norm_into(x_ref, g_ref, out_ref):
    sq = jnp.zeros((96, 128), jnp.float32)
    for c in range(24):
        xc = x_ref[:, c * 128:(c + 1) * 128].astype(jnp.float32)
        sq = sq + xc * xc
    inv = lax.rsqrt(jnp.sum(sq, axis=-1, keepdims=True) * (1.0 / 3072.0) + NORM_EPS)
    for c in range(24):
        xc = x_ref[:, c * 128:(c + 1) * 128].astype(jnp.float32)
        out_ref[:, c * 128:(c + 1) * 128] = (xc * inv * g_ref[c:c + 1, :].astype(jnp.float32)).astype(jnp.bfloat16)


def rope(h, cos_a, sin_a):
    return (h * cos_a + pltpu.roll(h, 64, 1) * sin_a).astype(jnp.bfloat16).astype(jnp.float32)


def cache_kernel(seq_ref, x_ref, g_ref, freq_ref, kin, vin, wk, wv, kout, vout, cos_ref, sin_ref,
                 wbuf, kbuf, vbuf, u_scr, new_scr, wsem, csem, osem):
    sp = lax.axis_index("sp")
    wcopies = [pltpu.make_async_copy(w, wbuf.at[i], wsem.at[i]) for i, w in enumerate((wk, wv))]
    ccopies = [pltpu.make_async_copy(kin, kbuf, csem.at[0]), pltpu.make_async_copy(vin, vbuf, csem.at[1])]
    for copy in (wcopies[0], ccopies[0], wcopies[1], ccopies[1]):
        copy.start()
    norm_into(x_ref, g_ref, u_scr)
    u = u_scr[...]

    sub = lax.broadcasted_iota(jnp.int32, (8, 128), 0)
    low = lax.broadcasted_iota(jnp.int32, (8, 128), 1) < 64
    for bg in range(12):
        pos = jnp.zeros((8, 128), jnp.int32)
        for j in range(8):
            pos = jnp.where(sub == j, seq_ref[bg * 8 + j], pos)
        angle = pos.astype(jnp.float32) * freq_ref[...]
        cos_ref[bg * 8:(bg + 1) * 8, :] = jnp.cos(angle)
        sin_a = jnp.sin(angle)
        sin_ref[bg * 8:(bg + 1) * 8, :] = jnp.where(low, -sin_a, sin_a)

    rowpos = lax.broadcasted_iota(jnp.int32, (64, 128), 0) // 4 + sp * 16

    def update(i, buf, turn, out):
        wcopies[i].wait()
        fresh = jnp.dot(u, wbuf[i], preferred_element_type=jnp.float32).astype(jnp.bfloat16).astype(jnp.float32)
        for kv in range(4):
            rows = fresh[:, kv * 128:(kv + 1) * 128]
            rows = rope(rows, cos_ref[...], sin_ref[...]) if turn else rows
            new_scr[pl.ds(kv, 96, stride=8), :] = rows
            new_scr[pl.ds(kv + 4, 96, stride=8), :] = rows
        ccopies[i].wait()

        @pl.loop(0, 12)
        def _(bg):
            for j in range(8):
                b = bg * 8 + j
                tile = new_scr[pl.ds(pl.multiple_of(b * 8, 8), 8), :]
                wide = jnp.broadcast_to(tile[None], (8, 8, 128)).reshape(64, 128)
                buf[b] = jnp.where(rowpos == seq_ref[b], wide, buf[b].astype(jnp.float32)).astype(jnp.bfloat16)
            pltpu.make_async_copy(buf.at[pl.ds(bg * 8, 8)], out.at[pl.ds(bg * 8, 8)], osem.at[i]).start()

    update(0, kbuf, True, kout)
    update(1, vbuf, False, vout)
    pltpu.make_async_copy(kbuf, kout, osem.at[0]).wait()
    pltpu.make_async_copy(vbuf, vout, osem.at[1]).wait()


def cache_part(seq_lens, x_tok, g_attn, k_blk, v_blk, wk, wv):
    inv_freq = np.power(ROPE_BASE, np.arange(64) * (-2.0 / 128)).astype(np.float32)
    freq = jnp.asarray(np.tile(inv_freq, (8, 2)))
    vmem = pl.BlockSpec(memory_space=pltpu.VMEM)
    hbm = pl.BlockSpec(memory_space=pl.ANY)
    cache = jax.ShapeDtypeStruct((96, 64, 128), jnp.bfloat16)
    table = jax.ShapeDtypeStruct((96, 128), jnp.float32)
    return pl.pallas_call(
        cache_kernel,
        out_shape=(cache, cache, table, table),
        in_specs=[pl.BlockSpec(memory_space=pltpu.SMEM), vmem, vmem, vmem, hbm, hbm, hbm, hbm],
        out_specs=(hbm, hbm, vmem, vmem),
        scratch_shapes=[
            pltpu.VMEM((2, 3072, 512), jnp.bfloat16),
            pltpu.VMEM((96, 64, 128), jnp.bfloat16),
            pltpu.VMEM((96, 64, 128), jnp.bfloat16),
            pltpu.VMEM((96, 3072), jnp.bfloat16),
            pltpu.VMEM((768, 128), jnp.float32),
            pltpu.SemaphoreType.DMA((2,)), pltpu.SemaphoreType.DMA((2,)), pltpu.SemaphoreType.DMA((2,)),
        ],
        compiler_params=pltpu.CompilerParams(vmem_limit_bytes=67043328),
        cost_estimate=pl.CostEstimate(flops=2 * 96 * 3072 * 1024, bytes_accessed=13_000_000, transcendentals=30_000),
        name="cache_part",
    )(seq_lens, x_tok, g_attn.reshape(24, 128), freq, k_blk.reshape(96, 64, 128), v_blk.reshape(96, 64, 128), wk, wv)


def main_kernel(seq_ref, x_ref, g1_ref, g2_ref, cos_ref, sin_ref, kout, vout, wq, wo, wg, wu, wd, y_ref,
                send, recv, mine, gath, fac, part, prem, u_scr, wbuf,
                send_sem, recv_sem, gsend_sem, grecv_sem, psend_sem, precv_sem, wsem, csem):
    me = lax.axis_index("sp")
    tp = lax.axis_index("tp")
    barrier = pltpu.get_barrier_semaphore()

    def turn_of(t):
        return lax.rem(lax.rem(t, 4) + lax.rem(lax.div(t, 4), 4) + lax.div(t, 16), 4)

    owner = turn_of(me) < 3
    my_own = lax.div(me, 4) * 3 + turn_of(me)

    def device_of(o):
        yz = lax.div(o, 3)
        return yz * 4 + lax.rem(lax.rem(o, 3) + 8 - lax.rem(yz, 4) - lax.div(yz, 4), 4)

    @pl.loop(1, N_SP)
    def _(j):
        pl.semaphore_signal(barrier, inc=1, device_id={"sp": lax.rem(me + j, N_SP)}, device_id_type=MESH)
    pl.semaphore_signal(barrier, inc=1, device_id={"tp": 1 - tp}, device_id_type=MESH)

    def cols(c):
        return pl.ds(pl.multiple_of(c * 512, 512), 512)

    def load(src, slot, rows):
        return pltpu.make_async_copy(src, wbuf.at[slot, rows], wsem.at[slot])

    def whole(src, c, slot):
        load(src.at[:, cols(c)], slot, pl.ds(0, 3072)).start()

    def start_wd(m):
        for third in range(3):
            piece = 3 * m + third
            n, kq = lax.div(piece, 4), lax.rem(piece, 4)
            load(wd.at[pl.ds(pl.multiple_of(kq * 1024, 1024), 1024), cols(n)], lax.rem(6 + m, SLOTS), pl.ds(third * 1024, 1024)).start()

    def arrived(slot):
        pltpu.make_async_copy(wbuf.at[slot], wbuf.at[slot], wsem.at[slot]).wait()

    def attend(kbuf, vbuf):
        kcopy = pltpu.make_async_copy(kout, kbuf, csem.at[0])
        vcopy = pltpu.make_async_copy(vout, vbuf, csem.at[1])
        for c in range(3):
            whole(wq, c, c)
        kcopy.start()
        vcopy.start()
        norm_into(x_ref, g1_ref, u_scr)
        for c in range(3):
            arrived(c)
            q = jnp.dot(u_scr[...], wbuf[c], preferred_element_type=jnp.float32).astype(jnp.bfloat16).astype(jnp.float32)
            for j in range(4):
                part[c, :, j * 128:(j + 1) * 128] = rope(q[:, j * 128:(j + 1) * 128], cos_ref[...], sin_ref[...])
            if c < 2:
                whole((wg, wu)[c], 5, c)
            else:
                whole(wg, 6, 2)
        for j in range(3):
            for half in range(2):
                load(wo.at[:, pl.ds((2 * j + half) * 512, 512)], 3 + j, pl.ds(half * 1536, 1536)).start()

        @pl.loop(0, 5)
        def _(c):
            whole(wg, c, 6 + 2 * c)
            whole(wu, c, 7 + 2 * c)

        kcopy.wait()
        vcopy.wait()

        col = lax.broadcasted_iota(jnp.int32, (8, 512), 1)
        sub = lax.broadcasted_iota(jnp.int32, (8, 512), 0)
        own_req = (col // 64) == sub
        colpos = (col % 64) // 4 + me * 16
        diag = lax.broadcasted_iota(jnp.int32, (96, 128), 0) == lax.broadcasted_iota(jnp.int32, (96, 128), 1)
        pl.semaphore_wait(barrier, N_SP)

        def attend_group(bg):
            rows = pl.ds(pl.multiple_of(bg * 8, 8), 8)
            q = jnp.concatenate([part[h // 4, rows, (h % 4) * 128:(h % 4 + 1) * 128] for h in range(12)], axis=0).astype(jnp.bfloat16)
            k = kbuf[rows].reshape(512, 128)
            v = vbuf[rows].reshape(512, 128)
            s = lax.dot_general(q, k, (((1,), (1,)), ((), ())), preferred_element_type=jnp.float32) * (128.0 ** -0.5)
            last = jnp.zeros((8, 512), jnp.int32)
            for j in range(8):
                last = jnp.where(sub == j, seq_ref[bg * 8 + j], last)
            ok = own_req & (colpos <= last)
            weights, tops, sums = [], [], []
            for kv in range(4):
                seen = ok & ((col % 4) == kv)
                for g in range(3):
                    h = kv * 3 + g
                    masked = jnp.where(seen, s[h * 8:(h + 1) * 8, :], -1e30)
                    top = jnp.max(masked, axis=-1, keepdims=True)
                    w = jnp.where(seen, jnp.exp(masked - top), 0.0)
                    weights.append(w)
                    tops.append(jnp.broadcast_to(top, (8, 128)))
                    sums.append(jnp.broadcast_to(jnp.sum(w, axis=-1, keepdims=True), (8, 128)))
            w = jnp.concatenate(weights, axis=0).astype(jnp.bfloat16)
            mix = jnp.dot(w, v, preferred_element_type=jnp.float32)
            top_row = jnp.sum(jnp.where(diag, jnp.concatenate(tops, axis=0), 0.0), axis=0, keepdims=True)
            sum_row = jnp.sum(jnp.where(diag, jnp.concatenate(sums, axis=0), 0.0), axis=0, keepdims=True)
            for kv in range(4):
                o = kv * 12 + bg
                send[o, 0:24, :] = mix[kv * 24:(kv + 1) * 24, :]
                send[o, 24:25, :] = top_row
                send[o, 25:26, :] = sum_row

        def send_group(bg):
            for kv in range(4):
                o = kv * 12 + bg
                t = device_of(o)

                @pl.when(t != me)
                def _():
                    pltpu.make_async_remote_copy(src_ref=send.at[o], dst_ref=recv.at[me], send_sem=send_sem, recv_sem=recv_sem,
                                                 device_id={"sp": t}, device_id_type=MESH).start()

        @pl.loop(0, 12 // 2)
        def _(step):
            groups = [lax.rem(step * 2 + i + me, 12) for i in range(2)]
            for bg in groups:
                attend_group(bg)
            for bg in groups:
                send_group(bg)

    pl.run_scoped(attend, pltpu.VMEM((96, 64, 128), jnp.bfloat16), pltpu.VMEM((96, 64, 128), jnp.bfloat16))

    @pl.when(owner)
    def _():
        recv[me] = send[my_own]
        pltpu.make_async_copy(recv.at[pl.ds(0, N_SP - 1)], recv.at[pl.ds(0, N_SP - 1)], recv_sem).wait()
        top = jnp.max(recv[:, 24, :], axis=0, keepdims=True)
        f = jnp.exp(recv[:, 24, :] - top)
        tot = jnp.sum(f * recv[:, 25, :], axis=0, keepdims=True)
        fac[...] = jnp.transpose(jnp.concatenate([f, jnp.broadcast_to(tot, (64, 128))], axis=0))
        ft = fac[pl.ds(pl.multiple_of(lax.div(my_own, 12) * 24, 8), 24), :]
        acc = [jnp.zeros((24, 128), jnp.float32) for _ in range(4)]
        for i in range(N_SP):
            acc[i % 4] = acc[i % 4] + recv[i, 0:24, :] * ft[:, i:i + 1]
        total = (acc[0] + acc[1]) + (acc[2] + acc[3])
        mine[...] = (total / ft[:, 64:65]).astype(jnp.bfloat16).astype(jnp.float32)
        gath[my_own] = mine[...]

        @pl.loop(1, N_SP)
        def _(j):
            pltpu.make_async_remote_copy(src_ref=mine, dst_ref=gath.at[my_own], send_sem=gsend_sem, recv_sem=grecv_sem,
                                         device_id={"sp": lax.rem(me + j, N_SP)}, device_id_type=MESH).start()
        pltpu.make_async_copy(gath.at[pl.ds(0, N_OWN - 1)], gath.at[pl.ds(0, N_OWN - 1)], grecv_sem).wait()

    @pl.when(jnp.logical_not(owner))
    def _():
        pltpu.make_async_copy(gath, gath, grecv_sem).wait()

    def exchange(phase, n):
        return pltpu.make_async_remote_copy(src_ref=part.at[n], dst_ref=prem.at[phase, n], send_sem=psend_sem.at[n],
                                            recv_sem=precv_sem.at[phase, n], device_id={"tp": 1 - tp}, device_id_type=MESH)

    def finish(attn, hid, act):
        for kv in range(4):
            for g in range(3):
                h = kv * 3 + g
                attn[:, h * 128:(h + 1) * 128] = gath[kv * 12:(kv + 1) * 12, g * 8:(g + 1) * 8, :].reshape(96, 128).astype(jnp.bfloat16)

        for j in range(3):
            arrived(3 + j)
            for half in range(2):
                n = 2 * j + half
                part[n] = jnp.dot(attn[...], wbuf[3 + j, half * 1536:(half + 1) * 1536, :], preferred_element_type=jnp.float32)
                exchange(0, n).start()
            if j == 0:
                whole(wu, 6, 3)
            else:
                whole((wg, wu)[j - 1], 7, 3 + j)
        sq = jnp.zeros((96, 128), jnp.float32)
        for n in range(6):
            exchange(0, n).wait_recv()
            for q in range(4):
                at = slice(n * 512 + q * 128, n * 512 + (q + 1) * 128)
                here = slice(q * 128, (q + 1) * 128)
                h = (x_ref[:, at].astype(jnp.float32) + (part[n, :, here] + prem[0, n, :, here])).astype(jnp.bfloat16)
                hid[:, at] = h
                h = h.astype(jnp.float32)
                sq = sq + h * h
        inv = lax.rsqrt(jnp.sum(sq, axis=-1, keepdims=True) * (1.0 / 3072.0) + NORM_EPS)
        for c in range(24):
            at = slice(c * 128, (c + 1) * 128)
            u_scr[:, at] = (hid[:, at].astype(jnp.float32) * inv * g2_ref[c:c + 1, :].astype(jnp.float32)).astype(jnp.bfloat16)

        @pl.loop(0, 8)
        def _(c):
            sg = lax.rem(6 + 2 * c, SLOTS)
            su = lax.rem(7 + 2 * c, SLOTS)
            arrived(sg)
            gate = jnp.dot(u_scr[...], wbuf[sg], preferred_element_type=jnp.float32).astype(jnp.bfloat16).astype(jnp.float32)
            arrived(su)
            up = jnp.dot(u_scr[...], wbuf[su], preferred_element_type=jnp.float32).astype(jnp.bfloat16).astype(jnp.float32)
            act[:, cols(c)] = (gate * lax.logistic(gate) * up).astype(jnp.bfloat16)

            @pl.when(c < 4)
            def _():
                start_wd(2 * c)
                start_wd(2 * c + 1)

        waited = -1
        for n in range(6):
            total = None
            for kq in range(4):
                m, third = divmod(n * 4 + kq, 3)
                if m > waited:
                    arrived((6 + m) % SLOTS)
                    waited = m
                d = jnp.dot(act[:, kq * 1024:(kq + 1) * 1024], wbuf[(6 + m) % SLOTS, third * 1024:(third + 1) * 1024, :], preferred_element_type=jnp.float32)
                total = d if total is None else total + d
            exchange(0, n).wait_send()
            part[n] = total
            exchange(1, n).start()
        for n in range(6):
            exchange(1, n).wait_recv()
            at = slice(n * 512, (n + 1) * 512)
            y_ref[:, at] = (hid[:, at].astype(jnp.float32) + (part[n] + prem[1, n])).astype(jnp.bfloat16)

    pl.run_scoped(finish, pltpu.VMEM((96, 1536), jnp.bfloat16), pltpu.VMEM((96, 3072), jnp.bfloat16), pltpu.VMEM((96, 4096), jnp.bfloat16))

    for n in range(6):
        exchange(1, n).wait_send()

    @pl.when(owner)
    def _():
        pltpu.make_async_copy(send.at[pl.ds(0, N_OWN - 1)], send.at[pl.ds(0, N_OWN - 1)], send_sem).wait()

        @pl.loop(1, N_SP)
        def _(j):
            pltpu.make_async_copy(mine, mine, gsend_sem).wait()

    @pl.when(jnp.logical_not(owner))
    def _():
        pltpu.make_async_copy(send, send, send_sem).wait()


def main_part(seq_lens, x_tok, g_attn, g_mlp, cos2, sin2, k_out, v_out, wq, wo, wg, wu, wd):
    vmem = pl.BlockSpec(memory_space=pltpu.VMEM)
    hbm = pl.BlockSpec(memory_space=pl.ANY)
    f32, bf16 = jnp.float32, jnp.bfloat16
    return pl.pallas_call(
        main_kernel,
        out_shape=jax.ShapeDtypeStruct((96, 3072), bf16),
        in_specs=[pl.BlockSpec(memory_space=pltpu.SMEM)] + [vmem] * 5 + [hbm] * 7,
        out_specs=vmem,
        scratch_shapes=[
            pltpu.VMEM((N_OWN, MSG, 128), f32),
            pltpu.VMEM((N_SP, MSG, 128), f32),
            pltpu.VMEM((24, 128), f32),
            pltpu.VMEM((N_OWN, 24, 128), f32),
            pltpu.VMEM((128, 128), f32),
            pltpu.VMEM((6, 96, 512), f32),
            pltpu.VMEM((2, 6, 96, 512), f32),
            pltpu.VMEM((96, 3072), bf16),
            pltpu.VMEM((SLOTS, 3072, 512), bf16),
            pltpu.SemaphoreType.DMA, pltpu.SemaphoreType.DMA, pltpu.SemaphoreType.DMA, pltpu.SemaphoreType.DMA,
            pltpu.SemaphoreType.DMA((6,)), pltpu.SemaphoreType.DMA((2, 6)), pltpu.SemaphoreType.DMA((SLOTS,)), pltpu.SemaphoreType.DMA((2,)),
        ],
        compiler_params=pltpu.CompilerParams(collective_id=1, has_side_effects=True, vmem_limit_bytes=67043328),
        cost_estimate=pl.CostEstimate(flops=2 * 96 * 47_000_000, bytes_accessed=100_000_000, transcendentals=1_000_000),
        name="main_part",
    )(seq_lens, x_tok, g_attn.reshape(24, 128), g_mlp.reshape(24, 128), cos2, sin2, k_out, v_out, wq, wo, wg, wu, wd)


def solution(mesh):
    cache_spec = P(None, "sp", "tp", None)
    col_spec = P(None, "tp")
    row_spec = P("tp", None)
    full_spec = P()

    def local_step(x_tok, seq_lens, k_blk, v_blk, g_attn, wq_loc, wk_loc, wv_loc, wo_loc, g_mlp, wg_loc, wu_loc, wd_loc):
        k_out, v_out, cos2, sin2 = cache_part(seq_lens, x_tok, g_attn, k_blk, v_blk, wk_loc, wv_loc)
        y_out = main_part(seq_lens, x_tok, g_attn, g_mlp, cos2, sin2, k_out, v_out, wq_loc, wo_loc, wg_loc, wu_loc, wd_loc)
        return y_out, k_out.reshape(k_blk.shape), v_out.reshape(v_blk.shape)

    return jax.shard_map(local_step, mesh=mesh, in_specs=(full_spec, full_spec, cache_spec, cache_spec, full_spec, col_spec, col_spec, col_spec, row_spec, full_spec, col_spec, col_spec, row_spec), out_specs=(full_spec, cache_spec, cache_spec), check_vma=False)
```

time: 450 us -> 68.9 us (0.15)
  waiting for transfers between devices: 203 us -> 0 us
  blocking collectives: 155 us -> 0 us
  Pallas kernels: 0 us -> 66.1 us
  matrix products: 51.7 us -> 0 us
  other arithmetic: 19 us -> 0 us
  between operations: 14.1 us -> 0.65 us
    psum x3 -> x0, waiting for transfers between devices: 203 us -> none  [the longest x1 152 us: local_step(): lax.psum(jnp.concatenate([blk_mix * factor, blk_sum * factor], axis=-1),...]
    pmax x1 -> x0, blocking collectives: 155 us -> none  [local_step(): glob_max = lax.pmax(blk_max, 'sp')]
    pallas_call x0 -> x2, Pallas kernels: none -> 66.1 us  [the longest x1 59.2 us: main_part(): pl.pallas_call(main_kernel, out_shape=jax.ShapeDtypeStruct((96, 3072), bf...]
    dot_general x8 -> x0, matrix products: 51.7 us -> none  [the longest x1 20.6 us: local_step(): jnp.dot(act_prod, wd_loc, preferred_element_type=jnp.float32)]
    select_n x1 -> x0, other arithmetic: 5.71 us -> none  [local_step(): v_out = jnp.where(is_new, v_new[:, None], v_blk)]
    reduce_sum x3 -> x0, other arithmetic: 4.97 us -> none  [the longest x2 2.88 us: rms_norm(): jnp.mean(x_f32 * x_f32, axis=-1, keepdims=True) + NORM_EPS]
  transfers between devices with their start and end apart: 3 -> 0, of which waited for: 3 -> 0; matrix products, arithmetic and copies ran while one was open for 0% -> 0% of each run, Pallas kernels for 0% -> 0%
where the time goes in v3:
time: 68.9 us; the launch traced here: 68.7 us
  Pallas kernels  66.1 us (96%)
  local copies, waits for them, and re-layouts  1.92 us (3%)
    pallas_call x1, Pallas kernels, main_part(): pl.pallas_call(main_kernel, out_shape=jax.ShapeDtypeStruct((96, 3072), bf...  59.2 us
    pallas_call x1, Pallas kernels, cache_part(): pl.pallas_call(cache_kernel, out_shape=(cache, cache, table, table), in_s...  6.93 us
    unnamed x1, local copies, waits for them, and re-layouts  1.92 us

profile of v3, /device:TPU:1, one launch (start us, length us, event | category | flops | bytes accessed | tf_op | source)
XLA Modules:
  0.0 68.7 jit_solution(13559795949953465400)
XLA Ops:
  0.6 6.9 %cache_part.1 = (bf16[96,64,128]{2,1,0:T(8,128)(2,1)}, bf16[96,64,128]{2,1,0:T(8,128)(2,1)}, f32[96,128]{1,0:T(8,128)}, f32[96,128]{1,0:T(8,128)}) custom-call(s32[96]{0:T(128)} %seq_ref.3, bf16[96,3072]{1,0:T(8,128)(2,1)} %x_ref.3, bf16[24,128]{1,0:T(8,128)(2,1)} %bitcast.10, f32[8,128]{1,0:T(8,128)} %constant.2.clone.freq_ref, ...), custom_call_target="tpu_custom_call" | custom-call | flops 603979776 | bytes 13000000 | tf_op jit(solution)/shard_map/cache_part/pallas_call | solution.py:88
  7.6 59.2 %main_part.1 = bf16[96,3072]{1,0:T(8,128)(2,1)} custom-call(s32[96]{0:T(128)} %seq_ref.3, bf16[96,3072]{1,0:T(8,128)(2,1)} %x_ref.3, bf16[24,128]{1,0:T(8,128)(2,1)} %bitcast.11, bf16[24,128]{1,0:T(8,128)(2,1)} %bitcast.12, f32[96,128]{1,0:T(8,128)} %get-tuple-element.7.cos_ref, f32[96,128]{1,0:T(8,128)} %get-tuple-element.8.sin_ref, ...), custom_call_target="tpu_custom_call" | custom-call | flops 9024000000 | bytes 100000000 | tf_op jit(solution)/shard_map/main_part/pallas_call | solution.py:350
  66.7 1.9 %copy.18 = bf16[96,3072]{1,0:T(8,128)(2,1)} copy(bf16[96,3072]{1,0:T(8,128)(2,1)} %main_part.1) | data formatting | bytes 1179648

commit v4 on v3

--- a/solution.py
+++ b/solution.py
@@ -106,7 +106,7 @@
 
 def main_kernel(seq_ref, x_ref, g1_ref, g2_ref, cos_ref, sin_ref, kout, vout, wq, wo, wg, wu, wd, y_ref,
                 send, recv, mine, gath, fac, part, prem, u_scr, wbuf,
-                send_sem, recv_sem, gsend_sem, grecv_sem, psend_sem, precv_sem, wsem, csem):
+                send_sem, recv_sem, gsend_sem, grecv_sem, psend_sem, precv_sem, wsem, csem, ysem):
     me = lax.axis_index("sp")
     tp = lax.axis_index("tp")
     barrier = pltpu.get_barrier_semaphore()
@@ -139,7 +139,7 @@
         for third in range(3):
             piece = 3 * m + third
             n, kq = lax.div(piece, 4), lax.rem(piece, 4)
-            load(wd.at[pl.ds(pl.multiple_of(kq * 1024, 1024), 1024), cols(n)], lax.rem(6 + m, SLOTS), pl.ds(third * 1024, 1024)).start()
+            load(wd.at[pl.ds(pl.multiple_of(kq * 1024, 1024), 1024), cols(n)], 5 + m, pl.ds(third * 1024, 1024)).start()
 
     def arrived(slot):
         pltpu.make_async_copy(wbuf.at[slot], wbuf.at[slot], wsem.at[slot]).wait()
@@ -231,37 +231,39 @@
 
     pl.run_scoped(attend, pltpu.VMEM((96, 64, 128), jnp.bfloat16), pltpu.VMEM((96, 64, 128), jnp.bfloat16))
 
-    @pl.when(owner)
-    def _():
-        recv[me] = send[my_own]
-        pltpu.make_async_copy(recv.at[pl.ds(0, N_SP - 1)], recv.at[pl.ds(0, N_SP - 1)], recv_sem).wait()
-        top = jnp.max(recv[:, 24, :], axis=0, keepdims=True)
-        f = jnp.exp(recv[:, 24, :] - top)
-        tot = jnp.sum(f * recv[:, 25, :], axis=0, keepdims=True)
-        fac[...] = jnp.transpose(jnp.concatenate([f, jnp.broadcast_to(tot, (64, 128))], axis=0))
-        ft = fac[pl.ds(pl.multiple_of(lax.div(my_own, 12) * 24, 8), 24), :]
-        acc = [jnp.zeros((24, 128), jnp.float32) for _ in range(4)]
-        for i in range(N_SP):
-            acc[i % 4] = acc[i % 4] + recv[i, 0:24, :] * ft[:, i:i + 1]
-        total = (acc[0] + acc[1]) + (acc[2] + acc[3])
-        mine[...] = (total / ft[:, 64:65]).astype(jnp.bfloat16).astype(jnp.float32)
-        gath[my_own] = mine[...]
-
-        @pl.loop(1, N_SP)
-        def _(j):
-            pltpu.make_async_remote_copy(src_ref=mine, dst_ref=gath.at[my_own], send_sem=gsend_sem, recv_sem=grecv_sem,
-                                         device_id={"sp": lax.rem(me + j, N_SP)}, device_id_type=MESH).start()
-        pltpu.make_async_copy(gath.at[pl.ds(0, N_OWN - 1)], gath.at[pl.ds(0, N_OWN - 1)], grecv_sem).wait()
-
-    @pl.when(jnp.logical_not(owner))
-    def _():
-        pltpu.make_async_copy(gath, gath, grecv_sem).wait()
-
     def exchange(phase, n):
         return pltpu.make_async_remote_copy(src_ref=part.at[n], dst_ref=prem.at[phase, n], send_sem=psend_sem.at[n],
                                             recv_sem=precv_sem.at[phase, n], device_id={"tp": 1 - tp}, device_id_type=MESH)
 
-    def finish(attn, hid, act):
+    def finish(attn, hid, act, extra):
+        pltpu.make_async_copy(wu.at[:, pl.ds(6 * 512, 512)], extra, wsem.at[SLOTS]).start()
+
+        @pl.when(owner)
+        def _():
+            recv[me] = send[my_own]
+            pltpu.make_async_copy(recv.at[pl.ds(0, N_SP - 1)], recv.at[pl.ds(0, N_SP - 1)], recv_sem).wait()
+            top = jnp.max(recv[:, 24, :], axis=0, keepdims=True)
+            f = jnp.exp(recv[:, 24, :] - top)
+            tot = jnp.sum(f * recv[:, 25, :], axis=0, keepdims=True)
+            fac[...] = jnp.transpose(jnp.concatenate([f, jnp.broadcast_to(tot, (64, 128))], axis=0))
+            ft = fac[pl.ds(pl.multiple_of(lax.div(my_own, 12) * 24, 8), 24), :]
+            acc = [jnp.zeros((24, 128), jnp.float32) for _ in range(4)]
+            for i in range(N_SP):
+                acc[i % 4] = acc[i % 4] + recv[i, 0:24, :] * ft[:, i:i + 1]
+            total = (acc[0] + acc[1]) + (acc[2] + acc[3])
+            mine[...] = (total / ft[:, 64:65]).astype(jnp.bfloat16).astype(jnp.float32)
+            gath[my_own] = mine[...]
+
+            @pl.loop(1, N_SP)
+            def _(j):
+                pltpu.make_async_remote_copy(src_ref=mine, dst_ref=gath.at[my_own], send_sem=gsend_sem, recv_sem=grecv_sem,
+                                             device_id={"sp": lax.rem(me + j, N_SP)}, device_id_type=MESH).start()
+            pltpu.make_async_copy(gath.at[pl.ds(0, N_OWN - 1)], gath.at[pl.ds(0, N_OWN - 1)], grecv_sem).wait()
+
+        @pl.when(jnp.logical_not(owner))
+        def _():
+            pltpu.make_async_copy(gath, gath, grecv_sem).wait()
+
         for kv in range(4):
             for g in range(3):
                 h = kv * 3 + g
@@ -273,10 +275,10 @@
                 n = 2 * j + half
                 part[n] = jnp.dot(attn[...], wbuf[3 + j, half * 1536:(half + 1) * 1536, :], preferred_element_type=jnp.float32)
                 exchange(0, n).start()
-            if j == 0:
-                whole(wu, 6, 3)
+            if j < 2:
+                whole((wg, wu)[j], 7, 3 + j)
             else:
-                whole((wg, wu)[j - 1], 7, 3 + j)
+                start_wd(0)
         sq = jnp.zeros((96, 128), jnp.float32)
         for n in range(6):
             exchange(0, n).wait_recv()
@@ -292,20 +294,28 @@
             at = slice(c * 128, (c + 1) * 128)
             u_scr[:, at] = (hid[:, at].astype(jnp.float32) * inv * g2_ref[c:c + 1, :].astype(jnp.float32)).astype(jnp.bfloat16)
 
-        @pl.loop(0, 8)
+        def gate_up(c, gate_ref, gate_sem, up_ref, up_sem):
+            pltpu.make_async_copy(gate_ref, gate_ref, wsem.at[gate_sem]).wait()
+            gate = jnp.dot(u_scr[...], gate_ref[...], preferred_element_type=jnp.float32).astype(jnp.bfloat16).astype(jnp.float32)
+            pltpu.make_async_copy(up_ref, up_ref, wsem.at[up_sem]).wait()
+            up = jnp.dot(u_scr[...], up_ref[...], preferred_element_type=jnp.float32).astype(jnp.bfloat16).astype(jnp.float32)
+            act[:, cols(c)] = (gate * lax.logistic(gate) * up).astype(jnp.bfloat16)
+
+        @pl.loop(0, 5)
         def _(c):
-            sg = lax.rem(6 + 2 * c, SLOTS)
-            su = lax.rem(7 + 2 * c, SLOTS)
-            arrived(sg)
-            gate = jnp.dot(u_scr[...], wbuf[sg], preferred_element_type=jnp.float32).astype(jnp.bfloat16).astype(jnp.float32)
-            arrived(su)
-            up = jnp.dot(u_scr[...], wbuf[su], preferred_element_type=jnp.float32).astype(jnp.bfloat16).astype(jnp.float32)
-            act[:, cols(c)] = (gate * lax.logistic(gate) * up).astype(jnp.bfloat16)
+            gate_up(c, wbuf.at[6 + 2 * c], 6 + 2 * c, wbuf.at[7 + 2 * c], 7 + 2 * c)
 
             @pl.when(c < 4)
             def _():
-                start_wd(2 * c)
                 start_wd(2 * c + 1)
+
+            @pl.when(c < 3)
+            def _():
+                start_wd(2 * c + 2)
+
+        gate_up(5, wbuf.at[0], 0, wbuf.at[1], 1)
+        gate_up(6, wbuf.at[2], 2, extra, SLOTS)
+        gate_up(7, wbuf.at[3], 3, wbuf.at[4], 4)
 
         waited = -1
         for n in range(6):
@@ -313,19 +323,22 @@
             for kq in range(4):
                 m, third = divmod(n * 4 + kq, 3)
                 if m > waited:
-                    arrived((6 + m) % SLOTS)
+                    arrived(5 + m)
                     waited = m
-                d = jnp.dot(act[:, kq * 1024:(kq + 1) * 1024], wbuf[(6 + m) % SLOTS, third * 1024:(third + 1) * 1024, :], preferred_element_type=jnp.float32)
+                d = jnp.dot(act[:, kq * 1024:(kq + 1) * 1024], wbuf[5 + m, third * 1024:(third + 1) * 1024, :], preferred_element_type=jnp.float32)
                 total = d if total is None else total + d
             exchange(0, n).wait_send()
             part[n] = total
             exchange(1, n).start()
         for n in range(6):
             exchange(1, n).wait_recv()
-            at = slice(n * 512, (n + 1) * 512)
-            y_ref[:, at] = (hid[:, at].astype(jnp.float32) + (part[n] + prem[1, n])).astype(jnp.bfloat16)
-
-    pl.run_scoped(finish, pltpu.VMEM((96, 1536), jnp.bfloat16), pltpu.VMEM((96, 3072), jnp.bfloat16), pltpu.VMEM((96, 4096), jnp.bfloat16))
+            at = pl.ds(n * 512, 512)
+            hid[:, at] = (hid[:, at].astype(jnp.float32) + (part[n] + prem[1, n])).astype(jnp.bfloat16)
+            pltpu.make_async_copy(hid.at[:, at], y_ref.at[:, at], ysem).start()
+        pltpu.make_async_copy(hid, y_ref, ysem).wait()
+
+    pl.run_scoped(finish, pltpu.VMEM((96, 1536), jnp.bfloat16), pltpu.VMEM((96, 3072), jnp.bfloat16), pltpu.VMEM((96, 4096), jnp.bfloat16),
+                  pltpu.VMEM((3072, 512), jnp.bfloat16))
 
     for n in range(6):
         exchange(1, n).wait_send()
@@ -351,7 +364,7 @@
         main_kernel,
         out_shape=jax.ShapeDtypeStruct((96, 3072), bf16),
         in_specs=[pl.BlockSpec(memory_space=pltpu.SMEM)] + [vmem] * 5 + [hbm] * 7,
-        out_specs=vmem,
+        out_specs=hbm,
         scratch_shapes=[
             pltpu.VMEM((N_OWN, MSG, 128), f32),
             pltpu.VMEM((N_SP, MSG, 128), f32),
@@ -363,7 +376,7 @@
             pltpu.VMEM((96, 3072), bf16),
             pltpu.VMEM((SLOTS, 3072, 512), bf16),
             pltpu.SemaphoreType.DMA, pltpu.SemaphoreType.DMA, pltpu.SemaphoreType.DMA, pltpu.SemaphoreType.DMA,
-            pltpu.SemaphoreType.DMA((6,)), pltpu.SemaphoreType.DMA((2, 6)), pltpu.SemaphoreType.DMA((SLOTS,)), pltpu.SemaphoreType.DMA((2,)),
+            pltpu.SemaphoreType.DMA((6,)), pltpu.SemaphoreType.DMA((2, 6)), pltpu.SemaphoreType.DMA((SLOTS + 1,)), pltpu.SemaphoreType.DMA((2,)), pltpu.SemaphoreType.DMA,
         ],
         compiler_params=pltpu.CompilerParams(collective_id=1, has_side_effects=True, vmem_limit_bytes=67043328),
         cost_estimate=pl.CostEstimate(flops=2 * 96 * 47_000_000, bytes_accessed=100_000_000, transcendentals=1_000_000),

time: 68.9 us -> 67.9 us (0.985)
  Pallas kernels: 66.1 us -> 65.2 us
    pallas_call x1, Pallas kernels: 59.2 us -> 58.2 us  [main_part(): pl.pallas_call(main_kernel, out_shape=jax.ShapeDtypeStruct((96, 3072), bf...]
where the time goes in v4:
time: 67.9 us; the launch traced here: 67.7 us
  Pallas kernels  65.2 us (96%)
  local copies, waits for them, and re-layouts  1.92 us (3%)
    pallas_call x1, Pallas kernels, main_part(): pl.pallas_call(main_kernel, out_shape=jax.ShapeDtypeStruct((96, 3072), bf...  58.2 us
    pallas_call x1, Pallas kernels, cache_part(): pl.pallas_call(cache_kernel, out_shape=(cache, cache, table, table), in_s...  6.93 us
    unnamed x1, local copies, waits for them, and re-layouts  1.92 us

profile of v4, /device:TPU:1, one launch (start us, length us, event | category | flops | bytes accessed | tf_op | source)
XLA Modules:
  0.0 67.7 jit_solution(14832150385211525461)
XLA Ops:
  0.6 6.9 %cache_part.1 = (bf16[96,64,128]{2,1,0:T(8,128)(2,1)}, bf16[96,64,128]{2,1,0:T(8,128)(2,1)}, f32[96,128]{1,0:T(8,128)}, f32[96,128]{1,0:T(8,128)}) custom-call(s32[96]{0:T(128)} %seq_ref.3, bf16[96,3072]{1,0:T(8,128)(2,1)} %x_ref.3, bf16[24,128]{1,0:T(8,128)(2,1)} %bitcast.10, f32[8,128]{1,0:T(8,128)} %constant.2.clone.freq_ref, ...), custom_call_target="tpu_custom_call" | custom-call | flops 603979776 | bytes 13000000 | tf_op jit(solution)/shard_map/cache_part/pallas_call | solution.py:88
  7.6 58.2 %main_part.1 = bf16[96,3072]{1,0:T(8,128)(2,1)} custom-call(s32[96]{0:T(128)} %seq_ref.3, bf16[96,3072]{1,0:T(8,128)(2,1)} %x_ref.3, bf16[24,128]{1,0:T(8,128)(2,1)} %bitcast.11, bf16[24,128]{1,0:T(8,128)(2,1)} %bitcast.12, f32[96,128]{1,0:T(8,128)} %get-tuple-element.7.cos_ref, f32[96,128]{1,0:T(8,128)} %get-tuple-element.8.sin_ref, ...), custom_call_target="tpu_custom_call" | custom-call | flops 9024000000 | bytes 100000000 | tf_op jit(solution)/shard_map/main_part/pallas_call | solution.py:363
  65.8 1.9 %copy.18 = bf16[96,3072]{1,0:T(8,128)(2,1)} copy(bf16[96,3072]{1,0:T(8,128)(2,1)} %main_part.1) | data formatting | bytes 1179648

commit v5 on v4

--- a/solution.py
+++ b/solution.py
@@ -221,9 +221,9 @@
                     pltpu.make_async_remote_copy(src_ref=send.at[o], dst_ref=recv.at[me], send_sem=send_sem, recv_sem=recv_sem,
                                                  device_id={"sp": t}, device_id_type=MESH).start()
 
-        @pl.loop(0, 12 // 2)
+        @pl.loop(0, 12 // 3)
         def _(step):
-            groups = [lax.rem(step * 2 + i + me, 12) for i in range(2)]
+            groups = [lax.rem(step * 3 + i + me, 12) for i in range(3)]
             for bg in groups:
                 attend_group(bg)
             for bg in groups:

time: 67.9 us -> 68.4 us (level)
  no operation moved by 1% of the time
where the time goes in v5:
time: 68.4 us; the launch traced here: 68.2 us
  Pallas kernels  65.6 us (96%)
  local copies, waits for them, and re-layouts  1.92 us (3%)
    pallas_call x1, Pallas kernels, main_part(): pl.pallas_call(main_kernel, out_shape=jax.ShapeDtypeStruct((96, 3072), bf...  58.7 us
    pallas_call x1, Pallas kernels, cache_part(): pl.pallas_call(cache_kernel, out_shape=(cache, cache, table, table), in_s...  6.93 us
    unnamed x1, local copies, waits for them, and re-layouts  1.92 us

profile of v5, /device:TPU:1, one launch (start us, length us, event | category | flops | bytes accessed | tf_op | source)
XLA Modules:
  0.0 68.2 jit_solution(3411998062292657907)
XLA Ops:
  0.6 6.9 %cache_part.1 = (bf16[96,64,128]{2,1,0:T(8,128)(2,1)}, bf16[96,64,128]{2,1,0:T(8,128)(2,1)}, f32[96,128]{1,0:T(8,128)}, f32[96,128]{1,0:T(8,128)}) custom-call(s32[96]{0:T(128)} %seq_ref.3, bf16[96,3072]{1,0:T(8,128)(2,1)} %x_ref.3, bf16[24,128]{1,0:T(8,128)(2,1)} %bitcast.10, f32[8,128]{1,0:T(8,128)} %constant.2.clone.freq_ref, ...), custom_call_target="tpu_custom_call" | custom-call | flops 603979776 | bytes 13000000 | tf_op jit(solution)/shard_map/cache_part/pallas_call | solution.py:88
  7.6 58.7 %main_part.1 = bf16[96,3072]{1,0:T(8,128)(2,1)} custom-call(s32[96]{0:T(128)} %seq_ref.3, bf16[96,3072]{1,0:T(8,128)(2,1)} %x_ref.3, bf16[24,128]{1,0:T(8,128)(2,1)} %bitcast.11, bf16[24,128]{1,0:T(8,128)(2,1)} %bitcast.12, f32[96,128]{1,0:T(8,128)} %get-tuple-element.7.cos_ref, f32[96,128]{1,0:T(8,128)} %get-tuple-element.8.sin_ref, ...), custom_call_target="tpu_custom_call" | custom-call | flops 9024000000 | bytes 100000000 | tf_op jit(solution)/shard_map/main_part/pallas_call | solution.py:363
  66.3 1.9 %copy.18 = bf16[96,3072]{1,0:T(8,128)(2,1)} copy(bf16[96,3072]{1,0:T(8,128)(2,1)} %main_part.1) | data formatting | bytes 1179648
